TPU v7x, 8 devices: a whole 2x2x1 slice. The times are simulated.
8 devices in a mesh: batch: 1 (over z), row: 2 (over y), col: 4 (over x, core).
Axes of the slice: x: 2, y: 2, z: 1, core: 2. Of those that a mesh axis runs over, the one named last changes fastest.
Arguments:
- spd_blocks: float32 [16, 384, 6144], P(('batch', 'row'), None, 'col')
Outputs:
- output: float32 [16, 384, 6144], P(('batch', 'row'), None, 'col')
All inputs are finite; a program needn't handle non-finite values.
Results may differ from a plain program's by a relative error of at most 0.001.
Values are sent between devices in bfloat16 or wider.
A program may use at most 1 GiB of HBM per device.

v0:
```python
import functools
import jax
import jax.numpy as jnp
from jax import lax
from jax.sharding import PartitionSpec as P, NamedSharding


def transposed_panel(row_panel, row_id, col_id, row_devs, col_devs, row_skip, col_skip):
    row_blocks = row_panel.shape[0]
    blk_size = row_panel.shape[1]
    if row_devs >= col_devs:
        grid_ratio = row_devs // col_devs
        blk_shift = (row_skip * row_devs - col_skip * col_devs) // col_devs
        pick_mask = (jnp.arange(grid_ratio) == row_id // col_devs) & (row_id % col_devs == col_id)
        spread = (row_panel[:, None] * pick_mask.astype(jnp.bfloat16)[None, :, None, None]).reshape(row_blocks * grid_ratio, blk_size, blk_size)
        if blk_shift >= 0:
            spread = jnp.pad(spread, ((blk_shift, 0), (0, 0), (0, 0)))
        else:
            spread = spread[-blk_shift:]
    else:
        grid_ratio = col_devs // row_devs
        blk_shift = (col_skip * col_devs - row_skip * row_devs) // row_devs
        if blk_shift >= 0:
            shifted = row_panel[blk_shift:]
        else:
            shifted = jnp.pad(row_panel, ((-blk_shift, 0), (0, 0), (0, 0)))
        grouped = shifted.reshape(shifted.shape[0] // grid_ratio, grid_ratio, blk_size, blk_size)
        chosen = lax.dynamic_index_in_dim(grouped, col_id // row_devs, axis=1, keepdims=False)
        spread = jnp.where(row_id == col_id % row_devs, chosen, jnp.zeros_like(chosen))
    return lax.psum(spread, "row")


def solution(mesh):
    row_devs = mesh.shape["row"]
    col_devs = mesh.shape["col"]

    def factor_local(a_loc):
        row_blocks, blk_size, local_cols = a_loc.shape
        col_blocks = local_cols // blk_size
        blk_count = row_blocks * row_devs
        row_id = lax.axis_index("row")
        col_id = lax.axis_index("col")
        eye_blk = jnp.eye(blk_size, dtype=jnp.float32)

        def panel_step(step_idx, window):
            win_rows, win_cols = window.shape
            win_rblk = win_rows // blk_size
            row_skip = row_blocks - win_rblk
            col_skip = col_blocks - win_cols // blk_size
            own_col = col_id == step_idx % col_devs
            is_owner = own_col & (row_id == step_idx % row_devs)
            col_off = (step_idx // col_devs - col_skip) * blk_size
            col_blk = lax.dynamic_slice_in_dim(window, col_off, blk_size, axis=1)
            diag_blk = lax.dynamic_slice_in_dim(col_blk, (step_idx // row_devs - row_skip) * blk_size, blk_size, axis=0)
            diag_own = jnp.tril(jnp.linalg.cholesky(jnp.where(is_owner, diag_blk, eye_blk)))
            diag_fac = lax.psum(jnp.where(is_owner, diag_own, 0.0), "row")
            diag_fac = jnp.where(own_col, diag_fac, eye_blk)
            solved = lax.linalg.triangular_solve(diag_fac, col_blk, left_side=False, lower=True, transpose_a=True)
            row_ids = (row_skip + jnp.arange(win_rblk)) * row_devs + row_id
            below_mask = (row_ids > step_idx)[:, None, None]
            on_diag = (row_ids == step_idx)[:, None, None]
            solved_blocks = solved.reshape(win_rblk, blk_size, blk_size)
            prior_col = col_blk.reshape(win_rblk, blk_size, blk_size)
            new_col = jnp.where(below_mask, solved_blocks, jnp.where(on_diag, diag_fac[None], prior_col))
            new_col = jnp.where(own_col, new_col, prior_col).reshape(win_rows, blk_size)
            window = lax.dynamic_update_slice_in_dim(window, new_col, col_off, axis=1)
            row_panel = lax.psum(jnp.where(below_mask & own_col, solved_blocks, 0.0).astype(jnp.bfloat16), "col")
            col_panel = transposed_panel(row_panel, row_id, col_id, row_devs, col_devs, row_skip, col_skip)
            update = lax.dot_general(row_panel.reshape(win_rows, blk_size), col_panel.reshape(win_cols, blk_size), (((1,), (1,)), ((), ())), preferred_element_type=jnp.float32)
            return window - update

        work_mat = a_loc.reshape(row_blocks * blk_size, local_cols)
        phase_count = min(blk_count, 8)
        bounds = [(phase_idx * blk_count) // phase_count for phase_idx in range(phase_count + 1)]
        for phase_idx in range(phase_count):
            row_start = (bounds[phase_idx] // row_devs) * blk_size
            col_start = (bounds[phase_idx] // col_devs) * blk_size
            window = lax.fori_loop(bounds[phase_idx], bounds[phase_idx + 1], panel_step, work_mat[row_start:, col_start:])
            work_mat = lax.dynamic_update_slice(work_mat, window, (row_start, col_start))
        row_blk_ids = jnp.arange(row_blocks) * row_devs + row_id
        col_blk_ids = jnp.arange(col_blocks) * col_devs + col_id
        keep_mask = row_blk_ids[:, None, None, None] >= col_blk_ids[None, None, :, None]
        factor = jnp.where(keep_mask, work_mat.reshape(row_blocks, blk_size, col_blocks, blk_size), 0.0)
        return factor.reshape(row_blocks, blk_size, local_cols)

    blk_spec = P(("batch", "row"), None, "col")
    return jax.shard_map(factor_local, mesh=mesh, in_specs=(blk_spec,), out_specs=blk_spec, check_vma=False)
```

profile of v0, /device:TPU:7, one launch (start us, length us, event | category | flops | bytes accessed | tf_op | source)
XLA Modules:
  0.0 3940.6 jit_solution(11615271145700829554)
XLA Ops:
  25.9 586.6 %while.185 = (s32[]{:T(128)}, f32[3072,1536]{0,1:T(8,128)}, s32[]{:T(128)}, s32[]{:T(128)}, pred[]{:T(512)}, /*index=5*/s32[]{:T(128)}, s32[]{:T(128)}, s32[]{:T...) while((s32[]{:T(128)}, f32[3072,1536]{0,1:T(8,128)}, ...), condition=%wide.region_10.12_spmd.clone.clone, body=%wide.region_0.11_spmd.clone.clone.sunk | while | flops 7449788928 | bytes 263024720 | solution.py:78
  113.5 24.1 all-reduce.30.cloned.1.call-done
  145.0 29.5 custom-call.199
  221.5 26.8 all-reduce.32.cloned.1.call-done
  383.6 24.3 all-reduce.30.cloned.1.call-done
  415.3 29.5 custom-call.199
  491.9 26.8 all-reduce.32.cloned.1.call-done
  623.8 546.0 %while.187 = (s32[]{:T(128)}, f32[2688,1536]{0,1:T(8,128)}, s32[]{:T(128)}, s32[]{:T(128)}, pred[]{:T(512)}, /*index=5*/s32[]{:T(128)}, s32[]{:T(128)}, s32[]{:T...) while((s32[]{:T(128)}, f32[2688,1536]{0,1:T(8,128)}, ...), condition=%wide.region_15.17_spmd.clone.clone, body=%wide.region_11.16_spmd.clone.clone.sunk | while | flops 6541115904 | bytes 236971184 | solution.py:78
  687.7 24.3 all-reduce.36.cloned.1.call-done
  719.2 29.5 custom-call.203
  949.7 24.3 all-reduce.36.cloned.1.call-done
  982.3 29.5 custom-call.203
  1189.9 506.2 %while.189 = (s32[]{:T(128)}, f32[2304,1152]{0,1:T(8,128)}, s32[]{:T(128)}, s32[]{:T(128)}, pred[]{:T(512)}, /*index=5*/s32[]{:T(128)}, s32[]{:T(128)}, s32[]{:T...) while((s32[]{:T(128)}, f32[2304,1152]{0,1:T(8,128)}, ...), condition=%wide.region_20.22_spmd.clone.clone, body=%wide.region_16.21_spmd.clone.clone.sunk | while | flops 4951785984 | bytes 168351920 | solution.py:78
  1253.5 24.3 all-reduce.42.cloned.1.call-done
  1284.8 29.5 custom-call.207
  1495.5 24.3 all-reduce.42.cloned.1.call-done
  1526.8 29.5 custom-call.207
  1710.0 482.1 %while.191 = (s32[]{:T(128)}, f32[1920,1152]{0,1:T(8,128)}, s32[]{:T(128)}, s32[]{:T(128)}, pred[]{:T(512)}, /*index=5*/s32[]{:T(128)}, s32[]{:T(128)}, s32[]{:T...) while((s32[]{:T(128)}, f32[1920,1152]{0,1:T(8,128)}, ...), condition=%wide.region_25.27_spmd.clone.clone, body=%wide.region_21.26_spmd.clone.clone.sunk | while | flops 4156506624 | bytes 147016848 | solution.py:78
  1773.7 24.3 all-reduce.48.cloned.1.call-done
  1805.6 29.5 custom-call.211
  2005.0 24.3 all-reduce.48.cloned.1.call-done
  2037.9 29.5 custom-call.211
  2203.1 434.9 %while.193 = (s32[]{:T(128)}, f32[1536,768]{0,1:T(8,128)}, s32[]{:T(128)}, s32[]{:T(128)}, pred[]{:T(512)}, /*index=5*/s32[]{:T(128)}, s32[]{:T(128)}, s32[]{:T(...) while((s32[]{:T(128)}, f32[1536,768]{0,1:T(8,128)}, ...), condition=%wide.region_30.32_spmd.clone.clone, body=%wide.region_26.31_spmd.clone.clone.sunk | while | flops 2907357696 | bytes 109068488 | solution.py:78
  2267.0 24.3 all-reduce.54.cloned.1.call-done
  2298.5 29.5 custom-call.215
  2348.6 23.8 all-reduce.56.cloned.1.call-done
  2475.0 24.3 all-reduce.54.cloned.1.call-done
  2506.5 29.5 custom-call.215
  2556.5 23.8 all-reduce.56.cloned.1.call-done
  2643.3 518.3 %while.195 = (s32[]{:T(128)}, f32[1152,768]{0,1:T(8,128)S(1)}, s32[]{:T(128)}, s32[]{:T(128)}, pred[]{:T(512)}, /*index=5*/s32[]{:T(128)}, s32[]{:T(128)}, s32[]...) while((s32[]{:T(128)}, f32[1152,768]{0,1:T(8,128)S(1)}, ...), condition=%wide.region_35.37_spmd.clone.clone, body=%wide.region_31.36_spmd.clone.clone.sunk | while | flops 2225472000 | bytes 112244056 | solution.py:78
  2739.8 24.3 all-reduce.60.cloned.1.call-done
  2784.8 30.9 custom-call.219
  2990.6 24.3 all-reduce.60.cloned.1.call-done
  3036.6 30.9 custom-call.219
  3164.7 386.5 %while.197 = (s32[]{:T(128)}, f32[768,384]{0,1:T(8,128)}, s32[]{:T(128)}, s32[]{:T(128)}, pred[]{:T(512)}, /*index=5*/s32[]{:T(128)}, s32[]{:T(128)}, s32[]{:T(1...) while((s32[]{:T(128)}, f32[768,384]{0,1:T(8,128)}, ...), condition=%wide.region_40.42_spmd.clone.clone, body=%wide.region_36.41_spmd.clone.clone.sunk | while | flops 1316503936 | bytes 57255956 | solution.py:78
  3227.5 24.0 all-reduce.66.cloned.1.call-done
  3259.5 29.5 custom-call.223
  3298.7 27.7 all-reduce.68.cloned.1.call-done
  3412.8 23.8 all-reduce.66.cloned.1.call-done
  3444.6 29.5 custom-call.223
  3483.8 27.7 all-reduce.68.cloned.1.call-done
  3553.7 347.8 %while.199 = (s32[]{:T(128)}, f32[384,384]{0,1:T(8,128)S(1)}, s32[]{:T(128)}, s32[1]{0:T(128)}, s32[]{:T(128)}, /*index=5*/pred[]{:T(512)}, s32[]{:T(128)}, s32[...) while((s32[]{:T(128)}, f32[384,384]{0,1:T(8,128)S(1)}, ...), condition=%wide.region_45.47_spmd.clone.clone, body=%wide.region_41.46_spmd.clone.clone.sunk | while | flops 748454272 | bytes 28544764 | solution.py:78
  3615.2 23.9 all-reduce.72.cloned.1.call-done
  3645.5 29.5 custom-call.227
  3678.3 27.3 all-reduce.74.cloned.1.call-done
  3789.5 23.9 all-reduce.72.cloned.1.call-done
  3820.8 29.5 custom-call.227
  3853.6 25.5 all-reduce.74.cloned.1.call-done
  (1353 shorter events, 2783.4 us)
Async XLA Ops:
  49.5 88.1 %all-reduce.30.cloned.1.call-start = ((), (), s32[]{:S(2)}) async-start(), calls=%async_computation | async-start | bytes 1179648 | tf_op jit(solution)/shard_map/while/body/eval_jaxpr/psum | solution.py:56
  113.4 134.9 %all-reduce.32.cloned.1.call-start = ((), (), s32[]{:S(2)}) async-start(), calls=%async_computation.1 | async-start | bytes 4718592 | tf_op jit(solution)/shard_map/while/body/eval_jaxpr/psum | solution.py:67
  198.1 89.9 %all-reduce.34.cloned.1.call-start = ((), (), s32[]{:S(2)}) async-start(), calls=%async_computation.2 | async-start | bytes 2359296 | tf_op jit(solution)/shard_map/while/body/eval_jaxpr/psum | solution.py:30
  319.7 88.2 %all-reduce.30.cloned.1.call-start = ((), (), s32[]{:S(2)}) async-start(), calls=%async_computation | async-start | bytes 1179648 | tf_op jit(solution)/shard_map/while/body/eval_jaxpr/psum | solution.py:56
  383.5 135.2 %all-reduce.32.cloned.1.call-start = ((), (), s32[]{:S(2)}) async-start(), calls=%async_computation.1 | async-start | bytes 4718592 | tf_op jit(solution)/shard_map/while/body/eval_jaxpr/psum | solution.py:67
  468.4 89.9 %all-reduce.34.cloned.1.call-start = ((), (), s32[]{:S(2)}) async-start(), calls=%async_computation.2 | async-start | bytes 2359296 | tf_op jit(solution)/shard_map/while/body/eval_jaxpr/psum | solution.py:30
  623.8 88.2 %all-reduce.36.cloned.1.call-start = ((), (), s32[]{:S(2)}) async-start(), calls=%async_computation.3 | async-start | bytes 1179648 | tf_op jit(solution)/shard_map/while/body/eval_jaxpr/psum | solution.py:56
  687.6 129.2 %all-reduce.38.cloned.1.call-start = ((), (), s32[]{:S(2)}) async-start(), calls=%async_computation.4 | async-start | bytes 4128768 | tf_op jit(solution)/shard_map/while/body/eval_jaxpr/psum | solution.py:67
  770.3 86.7 %all-reduce.40.cloned.1.call-start = ((), (), s32[]{:S(2)}) async-start(), calls=%async_computation.5 | async-start | bytes 2359296 | tf_op jit(solution)/shard_map/while/body/eval_jaxpr/psum | solution.py:30
  885.8 88.2 %all-reduce.36.cloned.1.call-start = ((), (), s32[]{:S(2)}) async-start(), calls=%async_computation.3 | async-start | bytes 1179648 | tf_op jit(solution)/shard_map/while/body/eval_jaxpr/psum | solution.py:56
  949.6 128.4 %all-reduce.38.cloned.1.call-start = ((), (), s32[]{:S(2)}) async-start(), calls=%async_computation.4 | async-start | bytes 4128768 | tf_op jit(solution)/shard_map/while/body/eval_jaxpr/psum | solution.py:67
  1033.4 84.9 %all-reduce.40.cloned.1.call-start = ((), (), s32[]{:S(2)}) async-start(), calls=%async_computation.5 | async-start | bytes 2359296 | tf_op jit(solution)/shard_map/while/body/eval_jaxpr/psum | solution.py:30
  1189.9 87.9 %all-reduce.42.cloned.1.call-start = ((), (), s32[]{:S(2)}) async-start(), calls=%async_computation.6 | async-start | bytes 1179648 | tf_op jit(solution)/shard_map/while/body/eval_jaxpr/psum | solution.py:56
  1253.4 121.1 %all-reduce.44.cloned.1.call-start = ((), (), s32[]{:S(2)}) async-start(), calls=%async_computation.7 | async-start | bytes 3538944 | tf_op jit(solution)/shard_map/while/body/eval_jaxpr/psum | solution.py:67
  1333.8 73.6 %all-reduce.46.cloned.1.call-start = ((), (), s32[]{:S(2)}) async-start(), calls=%async_computation.8 | async-start | bytes 1769472 | tf_op jit(solution)/shard_map/while/body/eval_jaxpr/psum | solution.py:30
  1431.9 87.9 %all-reduce.42.cloned.1.call-start = ((), (), s32[]{:S(2)}) async-start(), calls=%async_computation.6 | async-start | bytes 1179648 | tf_op jit(solution)/shard_map/while/body/eval_jaxpr/psum | solution.py:56
  1495.5 121.1 %all-reduce.44.cloned.1.call-start = ((), (), s32[]{:S(2)}) async-start(), calls=%async_computation.7 | async-start | bytes 3538944 | tf_op jit(solution)/shard_map/while/body/eval_jaxpr/psum | solution.py:67
  1575.9 73.6 %all-reduce.46.cloned.1.call-start = ((), (), s32[]{:S(2)}) async-start(), calls=%async_computation.8 | async-start | bytes 1769472 | tf_op jit(solution)/shard_map/while/body/eval_jaxpr/psum | solution.py:30
  1710.0 88.0 %all-reduce.48.cloned.1.call-start = ((), (), s32[]{:S(2)}) async-start(), calls=%async_computation.9 | async-start | bytes 1179648 | tf_op jit(solution)/shard_map/while/body/eval_jaxpr/psum | solution.py:56
  1773.6 114.7 %all-reduce.50.cloned.1.call-start = ((), (), s32[]{:S(2)}) async-start(), calls=%async_computation.10 | async-start | bytes 2949120 | tf_op jit(solution)/shard_map/while/body/eval_jaxpr/psum | solution.py:67
  1850.9 70.6 %all-reduce.52.cloned.1.call-start = ((), (), s32[]{:S(2)}) async-start(), calls=%async_computation.11 | async-start | bytes 1769472 | tf_op jit(solution)/shard_map/while/body/eval_jaxpr/psum | solution.py:30
  1941.3 88.0 %all-reduce.48.cloned.1.call-start = ((), (), s32[]{:S(2)}) async-start(), calls=%async_computation.9 | async-start | bytes 1179648 | tf_op jit(solution)/shard_map/while/body/eval_jaxpr/psum | solution.py:56
  2004.9 113.9 %all-reduce.50.cloned.1.call-start = ((), (), s32[]{:S(2)}) async-start(), calls=%async_computation.10 | async-start | bytes 2949120 | tf_op jit(solution)/shard_map/while/body/eval_jaxpr/psum | solution.py:67
  2083.3 68.8 %all-reduce.52.cloned.1.call-start = ((), (), s32[]{:S(2)}) async-start(), calls=%async_computation.11 | async-start | bytes 1769472 | tf_op jit(solution)/shard_map/while/body/eval_jaxpr/psum | solution.py:30
  2203.1 88.2 %all-reduce.54.cloned.1.call-start = ((), (), s32[]{:S(2)}) async-start(), calls=%async_computation.12 | async-start | bytes 1179648 | tf_op jit(solution)/shard_map/while/body/eval_jaxpr/psum | solution.py:56
  2266.9 105.4 %all-reduce.56.cloned.1.call-start = ((), (), s32[]{:S(2)}) async-start(), calls=%async_computation.13 | async-start | bytes 2359296 | tf_op jit(solution)/shard_map/while/body/eval_jaxpr/psum | solution.py:67
  2340.2 58.7 %all-reduce.58.cloned.1.call-start = ((), (), s32[]{:S(2)}) async-start(), calls=%async_computation.14 | async-start | bytes 1179648 | tf_op jit(solution)/shard_map/while/body/eval_jaxpr/psum | solution.py:30
  2411.1 88.2 %all-reduce.54.cloned.1.call-start = ((), (), s32[]{:S(2)}) async-start(), calls=%async_computation.12 | async-start | bytes 1179648 | tf_op jit(solution)/shard_map/while/body/eval_jaxpr/psum | solution.py:56
  2474.9 105.4 %all-reduce.56.cloned.1.call-start = ((), (), s32[]{:S(2)}) async-start(), calls=%async_computation.13 | async-start | bytes 2359296 | tf_op jit(solution)/shard_map/while/body/eval_jaxpr/psum | solution.py:67
  2548.2 58.7 %all-reduce.58.cloned.1.call-start = ((), (), s32[]{:S(2)}) async-start(), calls=%async_computation.14 | async-start | bytes 1179648 | tf_op jit(solution)/shard_map/while/body/eval_jaxpr/psum | solution.py:30
  2643.3 120.8 %all-reduce.60.cloned.1.call-start = ((), (), s32[]{:S(2)}) async-start(), calls=%async_computation.15 | async-start | bytes 1179648 | tf_op jit(solution)/shard_map/while/body/eval_jaxpr/psum | solution.py:56
  2739.7 119.7 %all-reduce.62.cloned.1.call-start = ((), (), s32[]{:S(2)}) async-start(), calls=%async_computation.16 | async-start | bytes 1769472 | tf_op jit(solution)/shard_map/while/body/eval_jaxpr/psum | solution.py:67
  2828.8 57.8 %all-reduce.64.cloned.1.call-start = ((), (), s32[]{:S(2)}) async-start(), calls=%async_computation.17 | async-start | bytes 1179648 | tf_op jit(solution)/shard_map/while/body/eval_jaxpr/psum | solution.py:30
  2894.1 120.8 %all-reduce.60.cloned.1.call-start = ((), (), s32[]{:S(2)}) async-start(), calls=%async_computation.15 | async-start | bytes 1179648 | tf_op jit(solution)/shard_map/while/body/eval_jaxpr/psum | solution.py:56
  2990.5 118.9 %all-reduce.62.cloned.1.call-start = ((), (), s32[]{:S(2)}) async-start(), calls=%async_computation.16 | async-start | bytes 1769472 | tf_op jit(solution)/shard_map/while/body/eval_jaxpr/psum | solution.py:67
  3080.6 56.0 %all-reduce.64.cloned.1.call-start = ((), (), s32[]{:S(2)}) async-start(), calls=%async_computation.17 | async-start | bytes 1179648 | tf_op jit(solution)/shard_map/while/body/eval_jaxpr/psum | solution.py:30
  3164.7 86.8 %all-reduce.66.cloned.1.call-start = ((), (), s32[]{:S(2)}) async-start(), calls=%async_computation.18 | async-start | bytes 1179648 | tf_op jit(solution)/shard_map/while/body/eval_jaxpr/psum | solution.py:56
  3227.1 99.3 %all-reduce.68.cloned.1.call-start = ((), (), s32[]{:S(2)}) async-start(), calls=%async_computation.19 | async-start | bytes 1179648 | tf_op jit(solution)/shard_map/while/body/eval_jaxpr/psum | solution.py:67
  3298.7 48.5 %all-reduce.70.cloned.1.call-start = ((), (), s32[]{:S(2)}) async-start(), calls=%async_computation.20 | async-start | bytes 589824 | tf_op jit(solution)/shard_map/while/body/eval_jaxpr/psum | solution.py:30
  3350.0 86.6 %all-reduce.66.cloned.1.call-start = ((), (), s32[]{:S(2)}) async-start(), calls=%async_computation.18 | async-start | bytes 1179648 | tf_op jit(solution)/shard_map/while/body/eval_jaxpr/psum | solution.py:56
  3412.4 99.1 %all-reduce.68.cloned.1.call-start = ((), (), s32[]{:S(2)}) async-start(), calls=%async_computation.19 | async-start | bytes 1179648 | tf_op jit(solution)/shard_map/while/body/eval_jaxpr/psum | solution.py:67
  3483.8 48.6 %all-reduce.70.cloned.1.call-start = ((), (), s32[]{:S(2)}) async-start(), calls=%async_computation.20 | async-start | bytes 589824 | tf_op jit(solution)/shard_map/while/body/eval_jaxpr/psum | solution.py:30
  3553.8 85.4 %all-reduce.72.cloned.1.call-start = ((), (), s32[]{:S(2)}) async-start(), calls=%async_computation.21 | async-start | bytes 1179648 | tf_op jit(solution)/shard_map/while/body/eval_jaxpr/psum | solution.py:56
  3614.9 90.7 %all-reduce.74.cloned.1.call-start = ((), (), s32[]{:S(2)}) async-start(), calls=%async_computation.22 | async-start | bytes 589824 | tf_op jit(solution)/shard_map/while/body/eval_jaxpr/psum | solution.py:67
  3678.2 48.3 %all-reduce.76.cloned.1.call-start = ((), (), s32[]{:S(2)}) async-start(), calls=%async_computation.23 | async-start | bytes 589824 | tf_op jit(solution)/shard_map/while/body/eval_jaxpr/psum | solution.py:30
  3728.0 85.4 %all-reduce.72.cloned.1.call-start = ((), (), s32[]{:S(2)}) async-start(), calls=%async_computation.21 | async-start | bytes 1179648 | tf_op jit(solution)/shard_map/while/body/eval_jaxpr/psum | solution.py:56
  3789.2 89.9 %all-reduce.74.cloned.1.call-start = ((), (), s32[]{:S(2)}) async-start(), calls=%async_computation.22 | async-start | bytes 589824 | tf_op jit(solution)/shard_map/while/body/eval_jaxpr/psum | solution.py:67
  3853.6 46.4 %all-reduce.76.cloned.1.call-start = ((), (), s32[]{:S(2)}) async-start(), calls=%async_computation.23 | async-start | bytes 589824 | tf_op jit(solution)/shard_map/while/body/eval_jaxpr/psum | solution.py:30
  (49 other events, 484.2 us)
Sparse Core Ops, SparseCore 0:
  113.5 23.9 all-reduce.29
  198.2 50.0 all-reduce.31
  250.9 37.0 all-reduce.33
  383.6 24.2 all-reduce.29
  468.6 50.0 all-reduce.31
  521.3 37.0 all-reduce.33
  687.7 24.2 all-reduce.35
  770.5 46.3 all-reduce.37
  819.9 37.0 all-reduce.39
  949.7 24.2 all-reduce.35
  1033.5 44.4 all-reduce.37
  1081.1 37.0 all-reduce.39
  1253.5 24.2 all-reduce.41
  1333.9 40.5 all-reduce.43
  1376.9 30.5 all-reduce.45
  1495.6 24.2 all-reduce.41
  1576.0 40.5 all-reduce.43
  1618.9 30.5 all-reduce.45
  1773.8 24.2 all-reduce.47
  1851.1 37.1 all-reduce.49
  1891.0 30.4 all-reduce.51
  2005.0 24.2 all-reduce.47
  2083.4 35.3 all-reduce.49
  2121.5 30.4 all-reduce.51
  2267.1 24.2 all-reduce.53
  2340.3 32.0 all-reduce.55
  2374.5 24.3 all-reduce.57
  2475.0 24.2 all-reduce.53
  2548.3 31.9 all-reduce.55
  2582.5 24.3 all-reduce.57
  2739.9 24.2 all-reduce.59
  2828.9 30.4 all-reduce.61
  2861.7 24.7 all-reduce.63
  2990.6 24.2 all-reduce.59
  3080.7 28.6 all-reduce.61
  3111.7 24.7 all-reduce.63
  3227.2 24.2 all-reduce.65
  3298.8 27.5 all-reduce.67
  3328.5 18.5 all-reduce.69
  3412.5 24.0 all-reduce.65
  3483.9 27.5 all-reduce.67
  3513.8 18.5 all-reduce.69
  3615.0 24.0 all-reduce.71
  3678.4 27.1 all-reduce.73
  3707.7 18.7 all-reduce.75
  3789.3 24.0 all-reduce.71
  3853.7 25.3 all-reduce.73
  3881.2 18.7 all-reduce.75
where the time goes:
time: 3960 us; the launch traced here: 3940 us
  other arithmetic  1620 us (41%)
  waiting for transfers between devices  1050 us (27%)
  local copies, waits for them, and re-layouts  766 us (19%)
  matrix products  283 us (7%)
  loops' own time  200 us (5%)
    another operation x160, other arithmetic, panel_step(): jnp.linalg.cholesky(jnp.where(is_owner, diag_blk, eye_blk))  921 us
    another operation x62, other arithmetic, panel_step(): lax.linalg.triangular_solve(diag_fac, col_blk, left_side=False, lower=Tru...  507 us
    psum x16, waiting for transfers between devices, panel_step(): diag_fac = lax.psum(jnp.where(is_owner, diag_own, 0.0), 'row')  387 us
    psum x16, waiting for transfers between devices, panel_step(): lax.psum(jnp.where(below_mask & own_col, solved_blocks, 0.0).astype(jnp.b...  361 us
    psum x16, waiting for transfers between devices, transposed_panel(): return lax.psum(spread, 'row')  304 us
    while x122, local copies, waits for them, and re-layouts  294 us
    another operation x8, loops' own time, factor_local(): lax.fori_loop(bounds[phase_idx], bounds[phase_idx + 1], panel_step, work_...  198 us
    another operation x80, matrix products, panel_step(): lax.linalg.triangular_solve(diag_fac, col_blk, left_side=False, lower=Tru...  133 us
  transfers between devices with their start and end apart: 48, of which 48 were waited for; matrix products, arithmetic and copies ran while one was open for 9% of the time, Pallas kernels for 0%

commit v1 on v0

v1 whole, which is shorter than its diff:
```python
import functools
import jax
import jax.numpy as jnp
from jax import lax
from jax.experimental import pallas as pl
from jax.experimental.pallas import tpu as pltpu
from jax.sharding import PartitionSpec as P

F32 = jnp.float32
BF16 = jnp.bfloat16
NB = 16
BS = 384
SUB = 128
MESH = pl.DeviceIdType.MESH


def dot_hi(a, b, dims):
    return lax.dot_general(a, b, (dims, ((), ())), precision=lax.Precision.HIGHEST, preferred_element_type=F32)


def lane_splat(x, i):
    return jnp.broadcast_to(x[:, i:i + 1], (8, SUB))


def row_splat(ref, row):
    return jnp.broadcast_to(ref[row:row + 1, :], (8, SUB))


def factor_tile(d_ref, off, u_ref, w_ref, sc):
    lane = lax.broadcasted_iota(jnp.int32, (8, SUB), 1)
    sub = lax.broadcasted_iota(jnp.int32, (8, SUB), 0)
    n_oct = SUB // 8
    X = [d_ref[pl.ds(pl.multiple_of(off + 8 * t, 8), 8), pl.ds(off, SUB)] for t in range(n_oct)]
    nxt = [lane_splat(X[0], i) for i in range(8)]
    for t in range(n_oct):
        j = 8 * t
        o = 160 * (t % 2)
        rows = X[t]
        for i in range(8):
            sc[o + 8 * i:o + 8 * i + 8, :] = nxt[i]
        d = {(m, i): row_splat(sc, o + 8 * i + m) for i in range(8) for m in range(i, 8)}
        sc[o + 64:o + 72, :] = rows
        sc[o + 72:o + 80, :] = jnp.where(lane < j, rows, jnp.where(lane == sub + j, 1.0, 0.0))
        inv = [None] * 8
        low = {}
        for i in range(8):
            inv[i] = lax.rsqrt(d[i, i])
            for m in range(i + 1, 8):
                low[m, i] = d[m, i] * inv[i]
            for m in range(i + 1, 8):
                for n in range(i + 1, m + 1):
                    d[m, n] = d[m, n] - low[m, i] * low[n, i]

        def column(s):
            c = []
            for i in range(8):
                x = lane_splat(X[s], j + i)
                for p in range(i):
                    x = x - low[i, p] * c[p]
                c.append(x * inv[i])
            return c

        if t + 1 < n_oct:
            first = column(t + 1)
            nxt = [lane_splat(X[t + 1], j + 8 + m) for m in range(8)]
            for i in range(8):
                sc[o + 80 + 8 * i:o + 88 + 8 * i, :] = first[i]
            for i in range(8):
                for m in range(8):
                    nxt[m] = nxt[m] - first[i] * row_splat(sc, o + 80 + 8 * i + m)
        u = []
        w = []
        for i in range(8):
            x = row_splat(sc, o + 64 + i)
            y = row_splat(sc, o + 72 + i)
            for p in range(i):
                x = x - low[i, p] * u[p]
                y = y - low[i, p] * w[p]
            u.append(x * inv[i])
            w.append(y * inv[i])
        u8 = u[7]
        w8 = w[7]
        for i in range(7):
            u8 = jnp.where(sub == i, u[i], u8)
            w8 = jnp.where(sub == i, w[i], w8)
        u_ref[j:j + 8, :] = jnp.where(lane >= sub + j, u8, 0.0)
        w_ref[j:j + 8, :] = jnp.where(lane < j + 8, w8, 0.0)
        z = [jnp.where(lane < j + 8, w[i], u[i]) for i in range(8)]
        for s in range(t + 1, n_oct):
            c = first if s == t + 1 else column(s)
            x = jnp.where((lane >= j) & (lane < j + 8), 0.0, X[s])
            for i in range(8):
                x = x - c[i] * z[i]
            X[s] = x


def kernel(a_hbm, o_hbm, S, PQ, FB, D, ub, wb, sc, ld_sem, st_sem, send_sem, p_sem, q_sem, fs_sem, fr_sem):
    g = lax.axis_index("batch")
    r = lax.axis_index("row")
    c = lax.axis_index("col")
    n_q0 = 64
    same = r == lax.rem(c, 2)

    def blk(s):
        return pl.ds(pl.multiple_of(s * BS, SUB), BS)

    def p_idx(k, t):
        return 8 * k - (k // 2) * ((k + 1) // 2) + t - (k + 1) // 2

    def q_idx(k, s):
        m = k // 4
        return 4 * k - (4 * (m * (m - 1) // 2) + (k - 4 * m) * m) + s - m

    def first_t(k):
        return (k + 2 - r) // 2

    def first_s(k):
        return (k + 4 - c) // 4

    def relay(k):
        return 2 - 2 * (lax.rem(k, 4) // 2)

    def to(row, col):
        return (g, row, col)

    def p_copy(k, t, kind, col):
        i = p_idx(k, t)
        return pltpu.make_async_remote_copy(PQ.at[i], PQ.at[i], send_sem.at[kind, i], p_sem.at[i],
                                            device_id=to(r, col), device_id_type=MESH)

    def q_copy(k, t):
        i = p_idx(k, t)
        q = q_idx(k, (2 * t + r - c) // 4)
        return pltpu.make_async_remote_copy(PQ.at[i], PQ.at[n_q0 + q], send_sem.at[2, i], q_sem.at[q],
                                            device_id=to(1 - r, c), device_id_type=MESH)

    def p_local(k, t):
        i = p_idx(k, t)
        return pltpu.make_async_remote_copy(PQ.at[i], PQ.at[i], send_sem.at[0, i], p_sem.at[i],
                                            device_id=to(r, c ^ 1), device_id_type=MESH)

    def q_local(k, s):
        q = q_idx(k, s)
        return pltpu.make_async_remote_copy(PQ.at[n_q0 + q], PQ.at[n_q0 + q], send_sem.at[2, 0], q_sem.at[q],
                                            device_id=to(1 - r, c), device_id_type=MESH)

    def each_send(k, t, act):
        kc = lax.rem(k, 4)
        i = 2 * t + r
        odd = lax.rem(k, 2)
        far = i > k + 1
        own = c == kc

        @pl.when(own & (far | (odd == 0)))
        def _():
            act(p_copy(k, t, 0, c ^ 1))

        @pl.when(own & (far | (odd == 1)))
        def _():
            act(p_copy(k, t, 1, relay(k)))

        @pl.when((c == relay(k)) & far)
        def _():
            act(p_copy(k, t, 0, c ^ 1))

        @pl.when(same & (lax.rem(i, 4) == c) & (own | far | (c == lax.rem(k + 1, 4))))
        def _():
            act(q_copy(k, t))

    def recv(k, t):
        p_local(k, t).wait_recv()
        each_send(k, t, lambda cp: cp.start())

    def col_index(k, s):
        return jnp.where(same, p_idx(k, 2 * s + (c - r) // 2), n_q0 + q_idx(k, s))

    def update(k, t, s):
        prod = lax.dot_general(PQ[p_idx(k, t)], PQ[col_index(k, s)], (((1,), (1,)), ((), ())),
                               preferred_element_type=F32)
        S[t, :, blk(s)] = S[t, :, blk(s)] - prod

    def fb_copy(slot, b):
        view = FB.at[slot, b, :, SUB * b:BS]
        return pltpu.make_async_remote_copy(view, view, fs_sem.at[slot, b], fr_sem.at[slot, b],
                                            device_id=to(1 - r, c), device_id_type=MESH)

    def load(t, s):
        return pltpu.make_async_copy(a_hbm.at[t, :, blk(s)], S.at[t, :, blk(s)], ld_sem.at[t, s])

    def store(t, s):
        return pltpu.make_async_copy(S.at[t, :, blk(s)], o_hbm.at[t, :, blk(s)], st_sem.at[t, s])

    def lower(t, s):
        return 2 * t + r >= 4 * s + c

    barrier = pltpu.get_barrier_semaphore()

    def all_blocks(fn):
        def body(n, _):
            fn(n // 4, lax.rem(n, 4))
            return 0
        lax.fori_loop(0, 32, body, 0)

    def begin(t, s):
        @pl.when(lower(t, s))
        def _():
            load(t, s).start()

    def blank(t, s):
        @pl.when(jnp.logical_not(lower(t, s)))
        def _():
            S[t, :, blk(s)] = jnp.zeros((BS, BS), F32)
            store(t, s).start()

    def arrived(t, s):
        @pl.when(lower(t, s))
        def _():
            load(t, s).wait()

    all_blocks(begin)
    for step in range(1, 8):
        dr, dc = step // 4, step % 4
        pl.semaphore_signal(barrier, inc=1, device_id=to(r ^ dr, c ^ dc), device_id_type=MESH)
    all_blocks(blank)
    pl.semaphore_wait(barrier, 7)
    all_blocks(arrived)

    def factor_diag(slot):
        def tile(b, _):
            off = pl.multiple_of(b * SUB, SUB)
            factor_tile(D, off, ub.at[b], wb, sc)
            w = wb[...]
            FB[slot, b, :, pl.ds(off, SUB)] = w

            @pl.when(b == 0)
            def _():
                rest = dot_hi(w, D[0:SUB, SUB:BS], ((1,), (0,)))
                FB[slot, 0, :, SUB:BS] = rest
                fb_copy(slot, 0).start()
                D[SUB:BS, SUB:BS] = D[SUB:BS, SUB:BS] - dot_hi(rest, rest, ((0,), (0,)))

            @pl.when(b == 1)
            def _():
                rest = dot_hi(w, D[SUB:2 * SUB, 2 * SUB:BS], ((1,), (0,)))
                FB[slot, 1, :, 2 * SUB:BS] = rest
                fb_copy(slot, 1).start()
                D[2 * SUB:BS, 2 * SUB:BS] = D[2 * SUB:BS, 2 * SUB:BS] - dot_hi(rest, rest, ((0,), (0,)))

            @pl.when(b == 2)
            def _():
                fb_copy(slot, 2).start()
            return 0
        lax.fori_loop(0, 3, tile, 0)

    def solve(k, t, s):
        x1 = dot_hi(S[t, :, pl.ds(pl.multiple_of(s * BS, SUB), SUB)], FB[s, 0, :, 0:SUB], ((1,), (1,)))
        s2 = S[t, :, pl.ds(pl.multiple_of(s * BS + SUB, SUB), SUB)] - dot_hi(x1, FB[s, 0, :, SUB:2 * SUB], ((1,), (0,)))
        x2 = dot_hi(s2, FB[s, 1, :, SUB:2 * SUB], ((1,), (1,)))
        s3 = S[t, :, pl.ds(pl.multiple_of(s * BS + 2 * SUB, SUB), SUB)] - dot_hi(x1, FB[s, 0, :, 2 * SUB:BS], ((1,), (0,)))
        s3 = s3 - dot_hi(x2, FB[s, 1, :, 2 * SUB:BS], ((1,), (0,)))
        x3 = dot_hi(s3, FB[s, 2, :, 2 * SUB:BS], ((1,), (1,)))
        i = p_idx(k, t)
        for n, x in enumerate((x1, x2, x3)):
            PQ[i, :, SUB * n:SUB * (n + 1)] = x.astype(BF16)
            S[t, :, pl.ds(pl.multiple_of(s * BS + SUB * n, SUB), SUB)] = x

    def body(k, _):
        kc = lax.rem(k, 4)
        kr = lax.rem(k, 2)
        sk = k // 4
        tk = k // 2
        own = c == kc
        t0 = first_t(k)

        @pl.when(own)
        def _():
            @pl.when(r == kr)
            def _():
                @pl.when(k > 0)
                def _():
                    recv(k - 1, tk)
                    update(k - 1, tk, sk)
                D[...] = S[tk, :, blk(sk)]
                factor_diag(sk)

            @pl.when((r != kr) & (k > 0))
            def _():
                q_local(k - 1, sk).wait_recv()

            def panel(t, _):
                @pl.when(k > 0)
                def _():
                    recv(k - 1, t)
                    update(k - 1, t, sk)

                @pl.when((r != kr) & (t == t0))
                def _():
                    for b in range(3):
                        fb_copy(sk, b).wait_recv()
                solve(k, t, sk)
                each_send(k, t, lambda cp: cp.start())
                store(t, sk).start()
                return 0
            lax.fori_loop(t0, 8, panel, 0)

            @pl.when((r != kr) & (t0 >= 8))
            def _():
                for b in range(3):
                    fb_copy(sk, b).wait_recv()

            @pl.when(r == kr)
            def _():
                for b in range(3):
                    S[tk, SUB * b:SUB * (b + 1), pl.ds(pl.multiple_of(sk * BS + SUB * b, SUB), SUB)] = ub[b].T
                    for e in range(b + 1, 3):
                        S[tk, SUB * e:SUB * (e + 1), pl.ds(pl.multiple_of(sk * BS + SUB * b, SUB), SUB)] = FB[sk, b, :, SUB * e:SUB * (e + 1)].T
                        S[tk, SUB * b:SUB * (b + 1), pl.ds(pl.multiple_of(sk * BS + SUB * e, SUB), SUB)] = jnp.zeros((SUB, SUB), F32)
                store(tk, sk).start()

        @pl.when(k > 0)
        def _():
            @pl.when((c != kc) & (c != lax.rem(k + 3, 4)))
            def _():
                lax.fori_loop(t0, 8, lambda t, _: (recv(k - 1, t), 0)[1], 0)
            s0 = first_s(k)

            @pl.when(jnp.logical_not(same))
            def _():
                lax.fori_loop(s0, 4, lambda s, _: (q_local(k - 1, s).wait_recv(), 0)[1], 0)

            def bulk(n, _):
                t = t0 + n // 4
                s = lax.rem(n, 4)

                @pl.when((s >= s0) & lower(t, s))
                def _():
                    update(k - 1, t, s)
                return 0
            lax.fori_loop(0, 4 * (8 - t0), bulk, 0)
        return 0

    lax.fori_loop(0, NB, body, 0)

    def drain(k, _):
        t0 = first_t(k)
        own = c == lax.rem(k, 4)
        nxt = c == lax.rem(k + 1, 4)

        def one(t, _):
            @pl.when(own | nxt | (2 * t + r > k + 1))
            def _():
                each_send(k, t, lambda cp: cp.wait_send())
            return 0
        lax.fori_loop(t0, 8, one, 0)

        @pl.when(own & (r == lax.rem(k, 2)))
        def _():
            for b in range(3):
                fb_copy(k // 4, b).wait_send()
        return 0
    lax.fori_loop(0, NB, drain, 0)
    all_blocks(lambda t, s: store(t, s).wait())


def solution(mesh):
    def local(a):
        return pl.pallas_call(
            kernel,
            out_shape=jax.ShapeDtypeStruct(a.shape, F32),
            in_specs=[pl.BlockSpec(memory_space=pl.ANY)],
            out_specs=pl.BlockSpec(memory_space=pl.ANY),
            scratch_shapes=[
                pltpu.VMEM((8, BS, 4 * BS), F32),
                pltpu.VMEM((104, BS, BS), BF16),
                pltpu.VMEM((4, 3, SUB, BS), F32),
                pltpu.VMEM((BS, BS), F32),
                pltpu.VMEM((3, SUB, SUB), F32),
                pltpu.VMEM((SUB, SUB), F32),
                pltpu.VMEM((320, SUB), F32),
                pltpu.SemaphoreType.DMA((8, 4)),
                pltpu.SemaphoreType.DMA((8, 4)),
                pltpu.SemaphoreType.DMA((3, 64)),
                pltpu.SemaphoreType.DMA((64,)),
                pltpu.SemaphoreType.DMA((40,)),
                pltpu.SemaphoreType.DMA((4, 3)),
                pltpu.SemaphoreType.DMA((4, 3)),
            ],
            compiler_params=pltpu.CompilerParams(collective_id=0, has_side_effects=True,
                                                 vmem_limit_bytes=67043328),
            name="cholesky",
        )(a)

    spec = P(("batch", "row"), None, "col")
    return jax.shard_map(local, mesh=mesh, in_specs=(spec,), out_specs=spec, check_vma=False)
```

time: 3960 us -> 380 us (0.10)
  other arithmetic: 1620 us -> 0 us
  waiting for transfers between devices: 1050 us -> 0 us
  local copies, waits for them, and re-layouts: 766 us -> 12.7 us
  Pallas kernels: 0 us -> 366 us
  matrix products: 283 us -> 0 us
  loops' own time: 200 us -> 0 us
    another operation x222 -> x0, other arithmetic: 1430 us -> none  [the longest x160 921 us: panel_step(): jnp.linalg.cholesky(jnp.where(is_owner, diag_blk, eye_blk))]
    psum x48 -> x0, waiting for transfers between devices: 1050 us -> none  [the longest x16 387 us: panel_step(): diag_fac = lax.psum(jnp.where(is_owner, diag_own, 0.0), 'row')]
    pallas_call x0 -> x1, Pallas kernels: none -> 366 us  [local(): pl.pallas_call(kernel, out_shape=jax.ShapeDtypeStruct(a.shape, F32), in_s...]
    while x122 -> x0, local copies, waits for them, and re-layouts: 294 us -> none
    another operation x24 -> x0, loops' own time: 200 us -> none  [the longest x8 198 us: factor_local(): lax.fori_loop(bounds[phase_idx], bounds[phase_idx + 1], panel_step, work_...]
    another operation x424 -> x0, local copies, waits for them, and re-layouts: 183 us -> none
    another operation x144 -> x0, matrix products: 162 us -> none  [the longest x80 133 us: panel_step(): lax.linalg.triangular_solve(diag_fac, col_blk, left_side=False, lower=Tru...]
    select_n x57 -> x0, other arithmetic: 128 us -> none  [the longest x12 62.1 us: panel_step(): new_col = jnp.where(own_col, new_col, prior_col).reshape(win_rows, blk_size)]
  transfers between devices with their start and end apart: 48 -> 0, of which waited for: 48 -> 0; matrix products, arithmetic and copies ran while one was open for 9% -> 0% of each run, Pallas kernels for 0% -> 0%
where the time goes in v1:
time: 380 us; the launch traced here: 379 us
  Pallas kernels  366 us (96%)
  local copies, waits for them, and re-layouts  12.7 us (3%)
    pallas_call x1, Pallas kernels, local(): pl.pallas_call(kernel, out_shape=jax.ShapeDtypeStruct(a.shape, F32), in_s...  366 us
    unnamed x1, local copies, waits for them, and re-layouts  12.7 us

profile of v1, /device:TPU:7, one launch (start us, length us, event | category | flops | bytes accessed | tf_op | source)
XLA Modules:
  0.0 378.7 jit_solution(984006344458103671)
XLA Ops:
  0.0 366.0 %cholesky.1 = f32[8,384,1536]{2,1,0:T(8,128)} custom-call(f32[8,384,1536]{2,1,0:T(8,128)} %a_hbm.1), custom_call_target="tpu_custom_call" | custom-call | tf_op jit(solution)/shard_map/cholesky/pallas_call | solution.py:367
  366.0 12.7 %copy.3 = f32[8,384,1536]{2,1,0:T(8,128)} copy(f32[8,384,1536]{2,1,0:T(8,128)} %cholesky.1) | data formatting | bytes 37748736

commit v2 on v1

--- a/solution.py
+++ b/solution.py
@@ -11,6 +11,9 @@
 NB = 16
 BS = 384
 SUB = 128
+MU = 4
+LAG = MU - 1
+HOP = MU // 2
 MESH = pl.DeviceIdType.MESH
 
 
@@ -94,7 +97,7 @@
             X[s] = x
 
 
-def kernel(a_hbm, o_hbm, S, PQ, FB, D, ub, wb, sc, ld_sem, st_sem, send_sem, p_sem, q_sem, fs_sem, fr_sem):
+def kernel(a_hbm, o_hbm, S, PQ, FB, D, ub, wb, sc, ld_sem, st_sem, send_sem, p_sem, q_sem, fs_sem, fr_sem, us_sem, ur_sem):
     g = lax.axis_index("batch")
     r = lax.axis_index("row")
     c = lax.axis_index("col")
@@ -114,12 +117,6 @@
     def first_t(k):
         return (k + 2 - r) // 2
 
-    def first_s(k):
-        return (k + 4 - c) // 4
-
-    def relay(k):
-        return 2 - 2 * (lax.rem(k, 4) // 2)
-
     def to(row, col):
         return (g, row, col)
 
@@ -130,9 +127,10 @@
 
     def q_copy(k, t):
         i = p_idx(k, t)
-        q = q_idx(k, (2 * t + r - c) // 4)
+        j = 2 * t + r
+        q = q_idx(k, j // 4)
         return pltpu.make_async_remote_copy(PQ.at[i], PQ.at[n_q0 + q], send_sem.at[2, i], q_sem.at[q],
-                                            device_id=to(1 - r, c), device_id_type=MESH)
+                                            device_id=to(1 - r, lax.rem(j, 4)), device_id_type=MESH)
 
     def p_local(k, t):
         i = p_idx(k, t)
@@ -146,35 +144,46 @@
 
     def each_send(k, t, act):
         kc = lax.rem(k, 4)
-        i = 2 * t + r
-        odd = lax.rem(k, 2)
-        far = i > k + 1
+        far = 2 * t + r > k + 1
         own = c == kc
 
-        @pl.when(own & (far | (odd == 0)))
-        def _():
+        @pl.when(own & far)
+        def _():
+            act(p_copy(k, t, 1, c ^ 3))
             act(p_copy(k, t, 0, c ^ 1))
 
-        @pl.when(own & (far | (odd == 1)))
-        def _():
-            act(p_copy(k, t, 1, relay(k)))
-
-        @pl.when((c == relay(k)) & far)
+        @pl.when(own)
+        def _():
+            act(q_copy(k, t))
+
+        @pl.when((c == (kc ^ 3)) & far)
         def _():
             act(p_copy(k, t, 0, c ^ 1))
 
-        @pl.when(same & (lax.rem(i, 4) == c) & (own | far | (c == lax.rem(k + 1, 4))))
-        def _():
-            act(q_copy(k, t))
+    def near_copy(k, n):
+        view = PQ.at[p_idx(k, (k + 1) // 2), :, SUB * n:SUB * (n + 1)]
+        return pltpu.make_async_remote_copy(view, view, us_sem.at[k, n], ur_sem.at[k, n],
+                                            device_id=to(r, lax.rem(k + 1, 4)), device_id_type=MESH)
+
+    def near_local(k, n):
+        view = PQ.at[p_idx(k, (k + 1) // 2), :, SUB * n:SUB * (n + 1)]
+        return pltpu.make_async_remote_copy(view, view, us_sem.at[k, n], ur_sem.at[k, n],
+                                            device_id=to(r, lax.rem(k, 4)), device_id_type=MESH)
 
     def recv(k, t):
         p_local(k, t).wait_recv()
-        each_send(k, t, lambda cp: cp.start())
+
+    def forward(k, t):
+        recv(k, t)
+        p_copy(k, t, 0, c ^ 1).start()
 
     def col_index(k, s):
         return jnp.where(same, p_idx(k, 2 * s + (c - r) // 2), n_q0 + q_idx(k, s))
 
     def update(k, t, s):
+        @pl.when(k == 0)
+        def _():
+            load(t, s).wait()
         prod = lax.dot_general(PQ[p_idx(k, t)], PQ[col_index(k, s)], (((1,), (1,)), ((), ())),
                                preferred_element_type=F32)
         S[t, :, blk(s)] = S[t, :, blk(s)] - prod
@@ -193,11 +202,9 @@
     def lower(t, s):
         return 2 * t + r >= 4 * s + c
 
-    barrier = pltpu.get_barrier_semaphore()
-
     def all_blocks(fn):
         def body(n, _):
-            fn(n // 4, lax.rem(n, 4))
+            fn(lax.rem(n, 8), n // 8)
             return 0
         lax.fori_loop(0, 32, body, 0)
 
@@ -206,26 +213,23 @@
         def _():
             load(t, s).start()
 
+    def blank_copy(t, s):
+        return pltpu.make_async_copy(S.at[0, :, 3 * BS:4 * BS], o_hbm.at[t, :, blk(s)], st_sem.at[t, s])
+
     def blank(t, s):
         @pl.when(jnp.logical_not(lower(t, s)))
         def _():
-            S[t, :, blk(s)] = jnp.zeros((BS, BS), F32)
-            store(t, s).start()
-
-    def arrived(t, s):
-        @pl.when(lower(t, s))
-        def _():
-            load(t, s).wait()
-
+            blank_copy(t, s).start()
+
+    barrier = pltpu.get_barrier_semaphore()
     all_blocks(begin)
     for step in range(1, 8):
         dr, dc = step // 4, step % 4
         pl.semaphore_signal(barrier, inc=1, device_id=to(r ^ dr, c ^ dc), device_id_type=MESH)
-    all_blocks(blank)
+    S[0, :, 3 * BS:4 * BS] = jnp.zeros((BS, BS), F32)
     pl.semaphore_wait(barrier, 7)
-    all_blocks(arrived)
-
-    def factor_diag(slot):
+
+    def factor_diag(slot, more):
         def tile(b, _):
             off = pl.multiple_of(b * SUB, SUB)
             factor_tile(D, off, ub.at[b], wb, sc)
@@ -236,127 +240,211 @@
             def _():
                 rest = dot_hi(w, D[0:SUB, SUB:BS], ((1,), (0,)))
                 FB[slot, 0, :, SUB:BS] = rest
-                fb_copy(slot, 0).start()
+                @pl.when(more)
+                def _():
+                    fb_copy(slot, 0).start()
                 D[SUB:BS, SUB:BS] = D[SUB:BS, SUB:BS] - dot_hi(rest, rest, ((0,), (0,)))
 
             @pl.when(b == 1)
             def _():
                 rest = dot_hi(w, D[SUB:2 * SUB, 2 * SUB:BS], ((1,), (0,)))
                 FB[slot, 1, :, 2 * SUB:BS] = rest
-                fb_copy(slot, 1).start()
+                @pl.when(more)
+                def _():
+                    fb_copy(slot, 1).start()
                 D[2 * SUB:BS, 2 * SUB:BS] = D[2 * SUB:BS, 2 * SUB:BS] - dot_hi(rest, rest, ((0,), (0,)))
 
             @pl.when(b == 2)
             def _():
-                fb_copy(slot, 2).start()
+                @pl.when(more)
+                def _():
+                    fb_copy(slot, 2).start()
             return 0
         lax.fori_loop(0, 3, tile, 0)
 
-    def solve(k, t, s):
-        x1 = dot_hi(S[t, :, pl.ds(pl.multiple_of(s * BS, SUB), SUB)], FB[s, 0, :, 0:SUB], ((1,), (1,)))
-        s2 = S[t, :, pl.ds(pl.multiple_of(s * BS + SUB, SUB), SUB)] - dot_hi(x1, FB[s, 0, :, SUB:2 * SUB], ((1,), (0,)))
-        x2 = dot_hi(s2, FB[s, 1, :, SUB:2 * SUB], ((1,), (1,)))
-        s3 = S[t, :, pl.ds(pl.multiple_of(s * BS + 2 * SUB, SUB), SUB)] - dot_hi(x1, FB[s, 0, :, 2 * SUB:BS], ((1,), (0,)))
-        s3 = s3 - dot_hi(x2, FB[s, 1, :, 2 * SUB:BS], ((1,), (0,)))
-        x3 = dot_hi(s3, FB[s, 2, :, 2 * SUB:BS], ((1,), (1,)))
-        i = p_idx(k, t)
-        for n, x in enumerate((x1, x2, x3)):
-            PQ[i, :, SUB * n:SUB * (n + 1)] = x.astype(BF16)
-            S[t, :, pl.ds(pl.multiple_of(s * BS + SUB * n, SUB), SUB)] = x
-
-    def body(k, _):
-        kc = lax.rem(k, 4)
-        kr = lax.rem(k, 2)
-        sk = k // 4
-        tk = k // 2
-        own = c == kc
-        t0 = first_t(k)
-
-        @pl.when(own)
-        def _():
-            @pl.when(r == kr)
-            def _():
-                @pl.when(k > 0)
-                def _():
-                    recv(k - 1, tk)
-                    update(k - 1, tk, sk)
-                D[...] = S[tk, :, blk(sk)]
-                factor_diag(sk)
-
-            @pl.when((r != kr) & (k > 0))
-            def _():
-                q_local(k - 1, sk).wait_recv()
-
-            def panel(t, _):
-                @pl.when(k > 0)
-                def _():
-                    recv(k - 1, t)
-                    update(k - 1, t, sk)
-
-                @pl.when((r != kr) & (t == t0))
-                def _():
-                    for b in range(3):
-                        fb_copy(sk, b).wait_recv()
-                solve(k, t, sk)
-                each_send(k, t, lambda cp: cp.start())
-                store(t, sk).start()
+    def solve(k, t, s, ready, done):
+        idx = p_idx(k, t)
+
+        def tile(n):
+            return pl.ds(pl.multiple_of(s * BS + SUB * n, SUB), SUB)
+
+        def put(n, x):
+            PQ[idx, :, SUB * n:SUB * (n + 1)] = x.astype(BF16)
+            S[t, :, tile(n)] = x
+            done(n)
+
+        ready(0)
+        x1 = dot_hi(S[t, :, tile(0)], FB[s, 0, :, 0:SUB], ((1,), (1,)))
+        put(0, x1)
+        rest = S[t, :, pl.ds(pl.multiple_of(s * BS + SUB, SUB), 2 * SUB)] - dot_hi(x1, FB[s, 0, :, SUB:BS], ((1,), (0,)))
+        ready(1)
+        x2 = dot_hi(rest[:, 0:SUB], FB[s, 1, :, SUB:2 * SUB], ((1,), (1,)))
+        put(1, x2)
+        last = rest[:, SUB:2 * SUB] - dot_hi(x2, FB[s, 1, :, 2 * SUB:BS], ((1,), (0,)))
+        ready(2)
+        put(2, dot_hi(last, FB[s, 2, :, 2 * SUB:BS], ((1,), (1,))))
+
+    def wave(n, _):
+        kd = n // MU
+        sd = kd // 4
+        td = kd // 2
+        diag = (lax.rem(n, MU) == 0) & (c == lax.rem(kd, 4)) & (r == lax.rem(kd, 2))
+
+        @pl.when(diag)
+        def _():
+            @pl.when(kd > 0)
+            def _():
+                @pl.when(kd == 1)
+                def _():
+                    load(td, sd).wait()
+                D[...] = S[td, :, blk(sd)]
+                idx = p_idx(kd - 1, td)
+                for e in range(3):
+                    near_local(kd - 1, e).wait_recv()
+                    part = PQ[idx, :, SUB * e:SUB * (e + 1)]
+                    D[...] = D[...] - lax.dot_general(part, part, (((1,), (1,)), ((), ())), preferred_element_type=F32)
+
+            @pl.when(kd == 0)
+            def _():
+                load(td, sd).wait()
+                D[...] = S[td, :, blk(sd)]
+            factor_diag(sd, kd < NB - 1)
+
+        near = (lax.rem(n, MU) == 1) & (c == lax.rem(kd, 4)) & (r == lax.rem(kd + 1, 2))
+
+        @pl.when(near)
+        def _():
+            t = (kd + 1) // 2
+
+            @pl.when(kd == 0)
+            def _():
+                load(t, sd).wait()
+
+            @pl.when(kd > 0)
+            def _():
+                @pl.when(lax.rem(kd, 2) == 1)
+                def _():
+                    recv(kd - 1, t)
+                update(kd - 1, t, sd)
+            solve(kd, t, sd, lambda e: fb_copy(sd, e).wait_recv(), lambda e: near_copy(kd, e).start())
+            each_send(kd, t, lambda cp: cp.start())
+            store(t, sd).start()
+
+        def span(v):
+            par = lax.rem(v + r, 2)
+            lo = (jnp.maximum(v - (NB - 1) + LAG - 1, 0) // LAG + 1 - par) // 2
+            hi = ((v + MU - 2) // MU + 1 - par) // 2
+            return par, lo, hi
+
+        @pl.when(n >= HOP)
+        def _():
+            v = n - HOP
+            par, lo, hi = span(v)
+
+            def pass_on(m, _):
+                k = 2 * m + par
+
+                @pl.when(c == (lax.rem(k, 4) ^ 3))
+                def _():
+                    forward(k, (v - LAG * k - r) // 2)
                 return 0
-            lax.fori_loop(t0, 8, panel, 0)
-
-            @pl.when((r != kr) & (t0 >= 8))
-            def _():
-                for b in range(3):
-                    fb_copy(sk, b).wait_recv()
-
-            @pl.when(r == kr)
-            def _():
-                for b in range(3):
-                    S[tk, SUB * b:SUB * (b + 1), pl.ds(pl.multiple_of(sk * BS + SUB * b, SUB), SUB)] = ub[b].T
-                    for e in range(b + 1, 3):
-                        S[tk, SUB * e:SUB * (e + 1), pl.ds(pl.multiple_of(sk * BS + SUB * b, SUB), SUB)] = FB[sk, b, :, SUB * e:SUB * (e + 1)].T
-                        S[tk, SUB * b:SUB * (b + 1), pl.ds(pl.multiple_of(sk * BS + SUB * e, SUB), SUB)] = jnp.zeros((SUB, SUB), F32)
-                store(tk, sk).start()
-
-        @pl.when(k > 0)
-        def _():
-            @pl.when((c != kc) & (c != lax.rem(k + 3, 4)))
-            def _():
-                lax.fori_loop(t0, 8, lambda t, _: (recv(k - 1, t), 0)[1], 0)
-            s0 = first_s(k)
+            lax.fori_loop(lo, hi, pass_on, 0)
+
+        @pl.when(n >= LAG)
+        def _():
+            v = n - LAG
+            par, lo, hi = span(v)
+            hi = hi - jnp.where(near & (kd > 0), 1, 0)
+
+            def arrive(m, _):
+                k = 2 * m + par
+                kc = lax.rem(k, 4)
+
+                @pl.when((c != kc) & (c != (kc ^ 3)))
+                def _():
+                    recv(k, (v - LAG * k - r) // 2)
+                return 0
+            lax.fori_loop(lo, hi, arrive, 0)
 
             @pl.when(jnp.logical_not(same))
             def _():
-                lax.fori_loop(s0, 4, lambda s, _: (q_local(k - 1, s).wait_recv(), 0)[1], 0)
-
-            def bulk(n, _):
-                t = t0 + n // 4
-                s = lax.rem(n, 4)
-
-                @pl.when((s >= s0) & lower(t, s))
-                def _():
-                    update(k - 1, t, s)
+                def arrive_q(s, _):
+                    j = 4 * s + c
+                    d = v - j
+
+                    @pl.when((d >= 0) & (lax.rem(d, LAG) == 0) & (d < LAG * j))
+                    def _():
+                        q_local(d // LAG, s).wait_recv()
+                    return 0
+                lax.fori_loop(0, 4, arrive_q, 0)
+
+            def apply(m, _):
+                k = 2 * m + par
+                i = v - LAG * k
+
+                def one(s, _):
+                    update(k, (i - r) // 2, s)
+                    return 0
+                lax.fori_loop((k + 4 - c) // 4, (i + 4 - c) // 4, one, 0)
                 return 0
-            lax.fori_loop(0, 4 * (8 - t0), bulk, 0)
+            lax.fori_loop(lo, hi, apply, 0)
+
+        @pl.when(lax.rem(n + c, 2) == r)
+        def _():
+            def task(m, _):
+                s = 3 - m
+                k = 4 * s + c
+                i = n - LAG * k
+
+                @pl.when((i > k + 1) & (i < NB))
+                def _():
+                    t = (i - r) // 2
+
+                    @pl.when(k == 0)
+                    def _():
+                        load(t, s).wait()
+                    solve(k, t, s, lambda e: None, lambda e: None)
+                    each_send(k, t, lambda cp: cp.start())
+                    store(t, s).start()
+                return 0
+            lax.fori_loop(0, 4, task, 0)
+
+        @pl.when(diag)
+        def _():
+            for b in range(3):
+                S[td, SUB * b:SUB * (b + 1), pl.ds(pl.multiple_of(sd * BS + SUB * b, SUB), SUB)] = ub[b].T
+                for e in range(b + 1, 3):
+                    S[td, SUB * e:SUB * (e + 1), pl.ds(pl.multiple_of(sd * BS + SUB * b, SUB), SUB)] = FB[sd, b, :, SUB * e:SUB * (e + 1)].T
+                    S[td, SUB * b:SUB * (b + 1), pl.ds(pl.multiple_of(sd * BS + SUB * e, SUB), SUB)] = jnp.zeros((SUB, SUB), F32)
+            store(td, sd).start()
+
+        @pl.when(n == 1)
+        def _():
+            all_blocks(blank)
         return 0
 
-    lax.fori_loop(0, NB, body, 0)
+    lax.fori_loop(0, MU * (NB - 1) + 1, wave, 0)
 
     def drain(k, _):
         t0 = first_t(k)
         own = c == lax.rem(k, 4)
-        nxt = c == lax.rem(k + 1, 4)
 
         def one(t, _):
-            @pl.when(own | nxt | (2 * t + r > k + 1))
-            def _():
-                each_send(k, t, lambda cp: cp.wait_send())
+            each_send(k, t, lambda cp: cp.wait_send())
             return 0
         lax.fori_loop(t0, 8, one, 0)
 
-        @pl.when(own & (r == lax.rem(k, 2)))
-        def _():
-            for b in range(3):
-                fb_copy(k // 4, b).wait_send()
+        @pl.when(own & (k < NB - 1))
+        def _():
+            @pl.when(r == lax.rem(k, 2))
+            def _():
+                for b in range(3):
+                    fb_copy(k // 4, b).wait_send()
+
+            @pl.when(r != lax.rem(k, 2))
+            def _():
+                for b in range(3):
+                    near_copy(k, b).wait_send()
         return 0
     lax.fori_loop(0, NB, drain, 0)
     all_blocks(lambda t, s: store(t, s).wait())
@@ -384,6 +472,8 @@
                 pltpu.SemaphoreType.DMA((40,)),
                 pltpu.SemaphoreType.DMA((4, 3)),
                 pltpu.SemaphoreType.DMA((4, 3)),
+                pltpu.SemaphoreType.DMA((16, 3)),
+                pltpu.SemaphoreType.DMA((16, 3)),
             ],
             compiler_params=pltpu.CompilerParams(collective_id=0, has_side_effects=True,
                                                  vmem_limit_bytes=67043328),

time: 380 us -> 312 us (0.82)
  Pallas kernels: 366 us -> 299 us
    pallas_call x1, Pallas kernels: 366 us -> 299 us  [local(): pl.pallas_call(kernel, out_shape=jax.ShapeDtypeStruct(a.shape, F32), in_s...]
where the time goes in v2:
time: 312 us; the launch traced here: 311 us
  Pallas kernels  299 us (96%)
  local copies, waits for them, and re-layouts  12.7 us (4%)
    pallas_call x1, Pallas kernels, local(): pl.pallas_call(kernel, out_shape=jax.ShapeDtypeStruct(a.shape, F32), in_s...  299 us
    unnamed x1, local copies, waits for them, and re-layouts  12.7 us

profile of v2, /device:TPU:7, one launch (start us, length us, event | category | flops | bytes accessed | tf_op | source)
XLA Modules:
  0.0 311.5 jit_solution(5520090612019312661)
XLA Ops:
  0.0 298.8 %cholesky.1 = f32[8,384,1536]{2,1,0:T(8,128)} custom-call(f32[8,384,1536]{2,1,0:T(8,128)} %a_hbm.1), custom_call_target="tpu_custom_call" | custom-call | tf_op jit(solution)/shard_map/cholesky/pallas_call | solution.py:455
  298.8 12.7 %copy.3 = f32[8,384,1536]{2,1,0:T(8,128)} copy(f32[8,384,1536]{2,1,0:T(8,128)} %cholesky.1) | data formatting | bytes 37748736

commit v3 on v2

--- a/solution.py
+++ b/solution.py
@@ -14,6 +14,7 @@
 MU = 4
 LAG = MU - 1
 HOP = MU // 2
+LAST = NB - 1
 MESH = pl.DeviceIdType.MESH
 
 
@@ -33,6 +34,7 @@
     lane = lax.broadcasted_iota(jnp.int32, (8, SUB), 1)
     sub = lax.broadcasted_iota(jnp.int32, (8, SUB), 0)
     n_oct = SUB // 8
+    half = n_oct // 2
     X = [d_ref[pl.ds(pl.multiple_of(off + 8 * t, 8), 8), pl.ds(off, SUB)] for t in range(n_oct)]
     nxt = [lane_splat(X[0], i) for i in range(8)]
     for t in range(n_oct):
@@ -63,7 +65,8 @@
                 c.append(x * inv[i])
             return c
 
-        if t + 1 < n_oct:
+        end = (t // half + 1) * half
+        if t + 1 < end:
             first = column(t + 1)
             nxt = [lane_splat(X[t + 1], j + 8 + m) for m in range(8)]
             for i in range(8):
@@ -89,12 +92,20 @@
         u_ref[j:j + 8, :] = jnp.where(lane >= sub + j, u8, 0.0)
         w_ref[j:j + 8, :] = jnp.where(lane < j + 8, w8, 0.0)
         z = [jnp.where(lane < j + 8, w[i], u[i]) for i in range(8)]
-        for s in range(t + 1, n_oct):
+        for s in range(t + 1, end):
             c = first if s == t + 1 else column(s)
             x = jnp.where((lane >= j) & (lane < j + 8), 0.0, X[s])
             for i in range(8):
                 x = x - c[i] * z[i]
             X[s] = x
+        if t + 1 == half:
+            e = 8 * half
+            top = u_ref[0:e, :]
+            z = jnp.where(lax.broadcasted_iota(jnp.int32, (e, SUB), 1) < e, w_ref[0:e, :], top)
+            prod = dot_hi(top[:, e:SUB], z, ((0,), (0,)))
+            for s in range(half, n_oct):
+                X[s] = jnp.where(lane < e, 0.0, X[s]) - prod[8 * (s - half):8 * (s - half + 1), :]
+            nxt = [lane_splat(X[half], e + m) for m in range(8)]
 
 
 def kernel(a_hbm, o_hbm, S, PQ, FB, D, ub, wb, sc, ld_sem, st_sem, send_sem, p_sem, q_sem, fs_sem, fr_sem, us_sem, ur_sem):
@@ -120,6 +131,10 @@
     def to(row, col):
         return (g, row, col)
 
+    def across(k):
+        kc = lax.rem(k, 4)
+        return jnp.where(lax.rem(kc, 2) == r, kc ^ 3, kc ^ 2)
+
     def p_copy(k, t, kind, col):
         i = p_idx(k, t)
         return pltpu.make_async_remote_copy(PQ.at[i], PQ.at[i], send_sem.at[kind, i], p_sem.at[i],
@@ -144,21 +159,27 @@
 
     def each_send(k, t, act):
         kc = lax.rem(k, 4)
-        far = 2 * t + r > k + 1
+        i = 2 * t + r
+        j = lax.rem(i, 4)
+        far = i > k + 1
         own = c == kc
 
         @pl.when(own & far)
         def _():
-            act(p_copy(k, t, 1, c ^ 3))
+            act(p_copy(k, t, 1, across(k)))
             act(p_copy(k, t, 0, c ^ 1))
 
-        @pl.when(own)
+        @pl.when(own & (i < LAST) & (jnp.logical_not(far) | (j // 2 == kc // 2)))
         def _():
             act(q_copy(k, t))
 
-        @pl.when((c == (kc ^ 3)) & far)
+        @pl.when((c == across(k)) & far)
         def _():
             act(p_copy(k, t, 0, c ^ 1))
+
+            @pl.when((i < LAST) & (j == (c ^ 1)))
+            def _():
+                act(q_copy(k, t))
 
     def near_copy(k, n):
         view = PQ.at[p_idx(k, (k + 1) // 2), :, SUB * n:SUB * (n + 1)]
@@ -175,7 +196,7 @@
 
     def forward(k, t):
         recv(k, t)
-        p_copy(k, t, 0, c ^ 1).start()
+        each_send(k, t, lambda cp: cp.start())
 
     def col_index(k, s):
         return jnp.where(same, p_idx(k, 2 * s + (c - r) // 2), n_q0 + q_idx(k, s))
@@ -310,6 +331,26 @@
                 D[...] = S[td, :, blk(sd)]
             factor_diag(sd, kd < NB - 1)
 
+        def span(v):
+            par = lax.rem(v + r, 2)
+            lo = (jnp.maximum(v - (NB - 1) + LAG - 1, 0) // LAG + 1 - par) // 2
+            hi = ((v + MU - 2) // MU + 1 - par) // 2
+            return par, lo, hi
+
+        @pl.when(n >= HOP)
+        def _():
+            v = n - HOP
+            par, lo, hi = span(v)
+
+            def pass_on(m, _):
+                k = 2 * m + par
+
+                @pl.when(c == across(k))
+                def _():
+                    forward(k, (v - LAG * k - r) // 2)
+                return 0
+            lax.fori_loop(lo, hi, pass_on, 0)
+
         near = (lax.rem(n, MU) == 1) & (c == lax.rem(kd, 4)) & (r == lax.rem(kd + 1, 2))
 
         @pl.when(near)
@@ -322,6 +363,8 @@
 
             @pl.when(kd > 0)
             def _():
+                q_local(kd - 1, sd).wait_recv()
+
                 @pl.when(lax.rem(kd, 2) == 1)
                 def _():
                     recv(kd - 1, t)
@@ -330,26 +373,6 @@
             each_send(kd, t, lambda cp: cp.start())
             store(t, sd).start()
 
-        def span(v):
-            par = lax.rem(v + r, 2)
-            lo = (jnp.maximum(v - (NB - 1) + LAG - 1, 0) // LAG + 1 - par) // 2
-            hi = ((v + MU - 2) // MU + 1 - par) // 2
-            return par, lo, hi
-
-        @pl.when(n >= HOP)
-        def _():
-            v = n - HOP
-            par, lo, hi = span(v)
-
-            def pass_on(m, _):
-                k = 2 * m + par
-
-                @pl.when(c == (lax.rem(k, 4) ^ 3))
-                def _():
-                    forward(k, (v - LAG * k - r) // 2)
-                return 0
-            lax.fori_loop(lo, hi, pass_on, 0)
-
         @pl.when(n >= LAG)
         def _():
             v = n - LAG
@@ -358,9 +381,8 @@
 
             def arrive(m, _):
                 k = 2 * m + par
-                kc = lax.rem(k, 4)
-
-                @pl.when((c != kc) & (c != (kc ^ 3)))
+
+                @pl.when((c != lax.rem(k, 4)) & (c != across(k)))
                 def _():
                     recv(k, (v - LAG * k - r) // 2)
                 return 0
@@ -370,9 +392,9 @@
             def _():
                 def arrive_q(s, _):
                     j = 4 * s + c
-                    d = v - j
-
-                    @pl.when((d >= 0) & (lax.rem(d, LAG) == 0) & (d < LAG * j))
+                    d = v - 1 - j
+
+                    @pl.when((j < LAST) & (d >= 0) & (lax.rem(d, LAG) == 0) & (d < LAG * (j - 1)))
                     def _():
                         q_local(d // LAG, s).wait_recv()
                     return 0

time: 312 us -> 277 us (0.89)
  Pallas kernels: 299 us -> 264 us
    pallas_call x1, Pallas kernels: 299 us -> 264 us  [local(): pl.pallas_call(kernel, out_shape=jax.ShapeDtypeStruct(a.shape, F32), in_s...]
where the time goes in v3:
time: 277 us
  Pallas kernels  264 us (95%)
  local copies, waits for them, and re-layouts  12.7 us (5%)
    pallas_call x1, Pallas kernels, local(): pl.pallas_call(kernel, out_shape=jax.ShapeDtypeStruct(a.shape, F32), in_s...  264 us
    unnamed x1, local copies, waits for them, and re-layouts  12.7 us

profile of v3, /device:TPU:7, one launch (start us, length us, event | category | flops | bytes accessed | tf_op | source)
XLA Modules:
  0.0 277.1 jit_solution(9261665973282058569)
XLA Ops:
  0.0 264.5 %cholesky.1 = f32[8,384,1536]{2,1,0:T(8,128)} custom-call(f32[8,384,1536]{2,1,0:T(8,128)} %a_hbm.1), custom_call_target="tpu_custom_call" | custom-call | tf_op jit(solution)/shard_map/cholesky/pallas_call | solution.py:477
  264.5 12.7 %copy.3 = f32[8,384,1536]{2,1,0:T(8,128)} copy(f32[8,384,1536]{2,1,0:T(8,128)} %cholesky.1) | data formatting | bytes 37748736

commit v4 on v3

--- a/solution.py
+++ b/solution.py
@@ -181,14 +181,18 @@
             def _():
                 act(q_copy(k, t))
 
+    def near_view(k, n):
+        i = p_idx(k, (k + 1) // 2)
+        if n < 2:
+            return PQ.at[i, :, SUB * n:SUB * (n + 1)]
+        return PQ.at[i, SUB * (n - 2):SUB * (n - 1), 2 * SUB:BS]
+
     def near_copy(k, n):
-        view = PQ.at[p_idx(k, (k + 1) // 2), :, SUB * n:SUB * (n + 1)]
-        return pltpu.make_async_remote_copy(view, view, us_sem.at[k, n], ur_sem.at[k, n],
+        return pltpu.make_async_remote_copy(near_view(k, n), near_view(k, n), us_sem.at[k, n], ur_sem.at[k, n],
                                             device_id=to(r, lax.rem(k + 1, 4)), device_id_type=MESH)
 
     def near_local(k, n):
-        view = PQ.at[p_idx(k, (k + 1) // 2), :, SUB * n:SUB * (n + 1)]
-        return pltpu.make_async_remote_copy(view, view, us_sem.at[k, n], ur_sem.at[k, n],
+        return pltpu.make_async_remote_copy(near_view(k, n), near_view(k, n), us_sem.at[k, n], ur_sem.at[k, n],
                                             device_id=to(r, lax.rem(k, 4)), device_id_type=MESH)
 
     def recv(k, t):
@@ -250,7 +254,13 @@
     S[0, :, 3 * BS:4 * BS] = jnp.zeros((BS, BS), F32)
     pl.semaphore_wait(barrier, 7)
 
-    def factor_diag(slot, more):
+    def bf_dot(x, y):
+        return lax.dot_general(x, y, (((1,), (1,)), ((), ())), preferred_element_type=F32)
+
+    def shrink(row, col, part):
+        D[row:row + SUB, col:BS] = D[row:row + SUB, col:BS] - bf_dot(part[row:row + SUB], part[col:BS])
+
+    def factor_diag(slot, more, late):
         def tile(b, _):
             off = pl.multiple_of(b * SUB, SUB)
             factor_tile(D, off, ub.at[b], wb, sc)
@@ -259,6 +269,7 @@
 
             @pl.when(b == 0)
             def _():
+                late()
                 rest = dot_hi(w, D[0:SUB, SUB:BS], ((1,), (0,)))
                 FB[slot, 0, :, SUB:BS] = rest
                 @pl.when(more)
@@ -283,7 +294,7 @@
             return 0
         lax.fori_loop(0, 3, tile, 0)
 
-    def solve(k, t, s, ready, done):
+    def solve(k, t, s, ready, done, pieces):
         idx = p_idx(k, t)
 
         def tile(n):
@@ -303,7 +314,13 @@
         put(1, x2)
         last = rest[:, SUB:2 * SUB] - dot_hi(x2, FB[s, 1, :, 2 * SUB:BS], ((1,), (0,)))
         ready(2)
-        put(2, dot_hi(last, FB[s, 2, :, 2 * SUB:BS], ((1,), (1,))))
+        rows = BS // pieces
+        for h in range(pieces):
+            at = slice(rows * h, rows * (h + 1))
+            x3 = dot_hi(last[at], FB[s, 2, :, 2 * SUB:BS], ((1,), (1,)))
+            PQ[idx, at, 2 * SUB:BS] = x3.astype(BF16)
+            S[t, at, tile(2)] = x3
+            done(2 + h)
 
     def wave(n, _):
         kd = n // MU
@@ -320,16 +337,30 @@
                     load(td, sd).wait()
                 D[...] = S[td, :, blk(sd)]
                 idx = p_idx(kd - 1, td)
-                for e in range(3):
+                for e in range(2):
                     near_local(kd - 1, e).wait_recv()
                     part = PQ[idx, :, SUB * e:SUB * (e + 1)]
-                    D[...] = D[...] - lax.dot_general(part, part, (((1,), (1,)), ((), ())), preferred_element_type=F32)
+                    for b in range(0, BS, SUB):
+                        shrink(b, b, part)
+                near_local(kd - 1, 2).wait_recv()
+                top = PQ[idx, 0:SUB, 2 * SUB:BS]
+                D[0:SUB, 0:SUB] = D[0:SUB, 0:SUB] - bf_dot(top, top)
 
             @pl.when(kd == 0)
             def _():
                 load(td, sd).wait()
                 D[...] = S[td, :, blk(sd)]
-            factor_diag(sd, kd < NB - 1)
+
+            def late():
+                @pl.when(kd > 0)
+                def _():
+                    for e in range(3, 5):
+                        near_local(kd - 1, e).wait_recv()
+                    part = PQ[p_idx(kd - 1, td), :, 2 * SUB:BS]
+                    shrink(0, SUB, part)
+                    shrink(SUB, SUB, part)
+                    shrink(2 * SUB, 2 * SUB, part)
+            factor_diag(sd, kd < NB - 1, late)
 
         def span(v):
             par = lax.rem(v + r, 2)
@@ -337,19 +368,21 @@
             hi = ((v + MU - 2) // MU + 1 - par) // 2
             return par, lo, hi
 
-        @pl.when(n >= HOP)
-        def _():
-            v = n - HOP
+        def pass_on(v):
             par, lo, hi = span(v)
 
-            def pass_on(m, _):
+            def one(m, _):
                 k = 2 * m + par
 
                 @pl.when(c == across(k))
                 def _():
                     forward(k, (v - LAG * k - r) // 2)
                 return 0
-            lax.fori_loop(lo, hi, pass_on, 0)
+            lax.fori_loop(lo, hi, one, 0)
+
+        @pl.when((n >= HOP) & ((lax.rem(n, MU) != 2) | (c != lax.rem(kd, 4)) | (r != lax.rem(kd + 1, 2))))
+        def _():
+            pass_on(n - HOP)
 
         near = (lax.rem(n, MU) == 1) & (c == lax.rem(kd, 4)) & (r == lax.rem(kd + 1, 2))
 
@@ -369,7 +402,12 @@
                 def _():
                     recv(kd - 1, t)
                 update(kd - 1, t, sd)
-            solve(kd, t, sd, lambda e: fb_copy(sd, e).wait_recv(), lambda e: near_copy(kd, e).start())
+
+            def ready(e):
+                if e == 1:
+                    pass_on(n + 1 - HOP)
+                fb_copy(sd, e).wait_recv()
+            solve(kd, t, sd, ready, lambda e: near_copy(kd, e).start(), 3)
             each_send(kd, t, lambda cp: cp.start())
             store(t, sd).start()
 
@@ -400,36 +438,48 @@
                     return 0
                 lax.fori_loop(0, 4, arrive_q, 0)
 
+        @pl.when(lax.rem(n + c, 2) == r)
+        def _():
+            def task(m, _):
+                s = 3 - m
+                k = 4 * s + c
+                i = n - LAG * k
+
+                @pl.when((i > k + 1) & (i < NB))
+                def _():
+                    t = (i - r) // 2
+
+                    @pl.when(k == 0)
+                    def _():
+                        load(t, s).wait()
+
+                    @pl.when(k > 0)
+                    def _():
+                        update(k - 1, t, s)
+                    solve(k, t, s, lambda e: None, lambda e: None, 1)
+                    each_send(k, t, lambda cp: cp.start())
+                    store(t, s).start()
+                return 0
+            lax.fori_loop(0, 4, task, 0)
+
+        @pl.when(n >= LAG)
+        def _():
+            v = n - LAG
+            par, lo, hi = span(v)
+            hi = hi - jnp.where(near & (kd > 0), 1, 0)
+
             def apply(m, _):
                 k = 2 * m + par
                 i = v - LAG * k
 
                 def one(s, _):
-                    update(k, (i - r) // 2, s)
+                    @pl.when(4 * s + c != k + 1)
+                    def _():
+                        update(k, (i - r) // 2, s)
                     return 0
                 lax.fori_loop((k + 4 - c) // 4, (i + 4 - c) // 4, one, 0)
                 return 0
             lax.fori_loop(lo, hi, apply, 0)
-
-        @pl.when(lax.rem(n + c, 2) == r)
-        def _():
-            def task(m, _):
-                s = 3 - m
-                k = 4 * s + c
-                i = n - LAG * k
-
-                @pl.when((i > k + 1) & (i < NB))
-                def _():
-                    t = (i - r) // 2
-
-                    @pl.when(k == 0)
-                    def _():
-                        load(t, s).wait()
-                    solve(k, t, s, lambda e: None, lambda e: None)
-                    each_send(k, t, lambda cp: cp.start())
-                    store(t, s).start()
-                return 0
-            lax.fori_loop(0, 4, task, 0)
 
         @pl.when(diag)
         def _():
@@ -465,7 +515,7 @@
 
             @pl.when(r != lax.rem(k, 2))
             def _():
-                for b in range(3):
+                for b in range(5):
                     near_copy(k, b).wait_send()
         return 0
     lax.fori_loop(0, NB, drain, 0)
@@ -494,8 +544,8 @@
                 pltpu.SemaphoreType.DMA((40,)),
                 pltpu.SemaphoreType.DMA((4, 3)),
                 pltpu.SemaphoreType.DMA((4, 3)),
-                pltpu.SemaphoreType.DMA((16, 3)),
-                pltpu.SemaphoreType.DMA((16, 3)),
+                pltpu.SemaphoreType.DMA((16, 5)),
+                pltpu.SemaphoreType.DMA((16, 5)),
             ],
             compiler_params=pltpu.CompilerParams(collective_id=0, has_side_effects=True,
                                                  vmem_limit_bytes=67043328),

time: 277 us -> 264 us (0.953)
  Pallas kernels: 264 us -> 251 us
    pallas_call x1, Pallas kernels: 264 us -> 251 us  [local(): pl.pallas_call(kernel, out_shape=jax.ShapeDtypeStruct(a.shape, F32), in_s...]
where the time goes in v4:
time: 264 us; the launch traced here: 263 us
  Pallas kernels  251 us (95%)
  local copies, waits for them, and re-layouts  12.7 us (5%)
    pallas_call x1, Pallas kernels, local(): pl.pallas_call(kernel, out_shape=jax.ShapeDtypeStruct(a.shape, F32), in_s...  251 us
    unnamed x1, local copies, waits for them, and re-layouts  12.7 us

profile of v4, /device:TPU:7, one launch (start us, length us, event | category | flops | bytes accessed | tf_op | source)
XLA Modules:
  0.0 263.4 jit_solution(4605402010694960786)
XLA Ops:
  0.0 250.7 %cholesky.1 = f32[8,384,1536]{2,1,0:T(8,128)} custom-call(f32[8,384,1536]{2,1,0:T(8,128)} %a_hbm.1), custom_call_target="tpu_custom_call" | custom-call | tf_op jit(solution)/shard_map/cholesky/pallas_call | solution.py:527
  250.7 12.7 %copy.3 = f32[8,384,1536]{2,1,0:T(8,128)} copy(f32[8,384,1536]{2,1,0:T(8,128)} %cholesky.1) | data formatting | bytes 37748736

commit v5 on v4

--- a/solution.py
+++ b/solution.py
@@ -108,7 +108,7 @@
             nxt = [lane_splat(X[half], e + m) for m in range(8)]
 
 
-def kernel(a_hbm, o_hbm, S, PQ, FB, D, ub, wb, sc, ld_sem, st_sem, send_sem, p_sem, q_sem, fs_sem, fr_sem, us_sem, ur_sem):
+def kernel(a_hbm, S, PQ, FB, D, ub, wb, sc, ld_sem, send_sem, p_sem, q_sem, fs_sem, fr_sem, us_sem, ur_sem):
     g = lax.axis_index("batch")
     r = lax.axis_index("row")
     c = lax.axis_index("col")
@@ -221,9 +221,6 @@
     def load(t, s):
         return pltpu.make_async_copy(a_hbm.at[t, :, blk(s)], S.at[t, :, blk(s)], ld_sem.at[t, s])
 
-    def store(t, s):
-        return pltpu.make_async_copy(S.at[t, :, blk(s)], o_hbm.at[t, :, blk(s)], st_sem.at[t, s])
-
     def lower(t, s):
         return 2 * t + r >= 4 * s + c
 
@@ -238,20 +235,16 @@
         def _():
             load(t, s).start()
 
-    def blank_copy(t, s):
-        return pltpu.make_async_copy(S.at[0, :, 3 * BS:4 * BS], o_hbm.at[t, :, blk(s)], st_sem.at[t, s])
-
     def blank(t, s):
         @pl.when(jnp.logical_not(lower(t, s)))
         def _():
-            blank_copy(t, s).start()
+            S[t, :, blk(s)] = jnp.zeros((BS, BS), F32)
 
     barrier = pltpu.get_barrier_semaphore()
     all_blocks(begin)
     for step in range(1, 8):
         dr, dc = step // 4, step % 4
         pl.semaphore_signal(barrier, inc=1, device_id=to(r ^ dr, c ^ dc), device_id_type=MESH)
-    S[0, :, 3 * BS:4 * BS] = jnp.zeros((BS, BS), F32)
     pl.semaphore_wait(barrier, 7)
 
     def bf_dot(x, y):
@@ -409,7 +402,6 @@
                 fb_copy(sd, e).wait_recv()
             solve(kd, t, sd, ready, lambda e: near_copy(kd, e).start(), 3)
             each_send(kd, t, lambda cp: cp.start())
-            store(t, sd).start()
 
         @pl.when(n >= LAG)
         def _():
@@ -458,7 +450,6 @@
                         update(k - 1, t, s)
                     solve(k, t, s, lambda e: None, lambda e: None, 1)
                     each_send(k, t, lambda cp: cp.start())
-                    store(t, s).start()
                 return 0
             lax.fori_loop(0, 4, task, 0)
 
@@ -488,9 +479,8 @@
                 for e in range(b + 1, 3):
                     S[td, SUB * e:SUB * (e + 1), pl.ds(pl.multiple_of(sd * BS + SUB * b, SUB), SUB)] = FB[sd, b, :, SUB * e:SUB * (e + 1)].T
                     S[td, SUB * b:SUB * (b + 1), pl.ds(pl.multiple_of(sd * BS + SUB * e, SUB), SUB)] = jnp.zeros((SUB, SUB), F32)
-            store(td, sd).start()
-
-        @pl.when(n == 1)
+
+        @pl.when(n == 2)
         def _():
             all_blocks(blank)
         return 0
@@ -519,25 +509,22 @@
                     near_copy(k, b).wait_send()
         return 0
     lax.fori_loop(0, NB, drain, 0)
-    all_blocks(lambda t, s: store(t, s).wait())
 
 
 def solution(mesh):
     def local(a):
         return pl.pallas_call(
             kernel,
-            out_shape=jax.ShapeDtypeStruct(a.shape, F32),
+            out_shape=pltpu.VMEM(a.shape, F32),
             in_specs=[pl.BlockSpec(memory_space=pl.ANY)],
-            out_specs=pl.BlockSpec(memory_space=pl.ANY),
+            out_specs=pl.BlockSpec(memory_space=pltpu.VMEM),
             scratch_shapes=[
-                pltpu.VMEM((8, BS, 4 * BS), F32),
                 pltpu.VMEM((104, BS, BS), BF16),
                 pltpu.VMEM((4, 3, SUB, BS), F32),
                 pltpu.VMEM((BS, BS), F32),
                 pltpu.VMEM((3, SUB, SUB), F32),
                 pltpu.VMEM((SUB, SUB), F32),
                 pltpu.VMEM((320, SUB), F32),
-                pltpu.SemaphoreType.DMA((8, 4)),
                 pltpu.SemaphoreType.DMA((8, 4)),
                 pltpu.SemaphoreType.DMA((3, 64)),
                 pltpu.SemaphoreType.DMA((64,)),
@@ -548,7 +535,7 @@
                 pltpu.SemaphoreType.DMA((16, 5)),
             ],
             compiler_params=pltpu.CompilerParams(collective_id=0, has_side_effects=True,
-                                                 vmem_limit_bytes=67043328),
+                                                 vmem_limit_bytes=44 * 2 ** 20),
             name="cholesky",
         )(a)
 

time: 264 us -> 257 us (0.973)
  local copies, waits for them, and re-layouts: 12.7 us -> 6.85 us
    unnamed x1, local copies, waits for them, and re-layouts: 12.7 us -> 6.85 us
where the time goes in v5:
time: 257 us
  Pallas kernels  250 us (97%)
  local copies, waits for them, and re-layouts  6.85 us (3%)
    pallas_call x1, Pallas kernels, local(): pl.pallas_call(kernel, out_shape=pltpu.VMEM(a.shape, F32), in_specs=[pl.B...  250 us
    unnamed x1, local copies, waits for them, and re-layouts  6.85 us

profile of v5, /device:TPU:7, one launch (start us, length us, event | category | flops | bytes accessed | tf_op | source)
XLA Modules:
  0.0 256.8 jit_solution(14133339711233320267)
XLA Ops:
  0.0 249.9 %cholesky.1 = f32[8,384,1536]{2,1,0:T(8,128)S(1)} custom-call(f32[8,384,1536]{2,1,0:T(8,128)} %a_hbm.1), custom_call_target="tpu_custom_call" | custom-call | tf_op jit(solution)/shard_map/cholesky/pallas_call | solution.py:516
  249.9 6.9 %copy.3 = f32[8,384,1536]{2,1,0:T(8,128)} copy(f32[8,384,1536]{2,1,0:T(8,128)S(1)} %cholesky.1) | data formatting | bytes 37748736

commit v6 on v5

--- a/solution.py
+++ b/solution.py
@@ -30,7 +30,7 @@
     return jnp.broadcast_to(ref[row:row + 1, :], (8, SUB))
 
 
-def factor_tile(d_ref, off, u_ref, w_ref, sc):
+def factor_tile(d_ref, off, u_ref, w_ref, sc, mid):
     lane = lax.broadcasted_iota(jnp.int32, (8, SUB), 1)
     sub = lax.broadcasted_iota(jnp.int32, (8, SUB), 0)
     n_oct = SUB // 8
@@ -44,8 +44,7 @@
         for i in range(8):
             sc[o + 8 * i:o + 8 * i + 8, :] = nxt[i]
         d = {(m, i): row_splat(sc, o + 8 * i + m) for i in range(8) for m in range(i, 8)}
-        sc[o + 64:o + 72, :] = rows
-        sc[o + 72:o + 80, :] = jnp.where(lane < j, rows, jnp.where(lane == sub + j, 1.0, 0.0))
+        sc[o + 64:o + 72, :] = jnp.where((lane >= j) & (lane < j + 8), jnp.where(lane == sub + j, 1.0, 0.0), rows)
         inv = [None] * 8
         low = {}
         for i in range(8):
@@ -74,24 +73,23 @@
             for i in range(8):
                 for m in range(8):
                     nxt[m] = nxt[m] - first[i] * row_splat(sc, o + 80 + 8 * i + m)
-        u = []
-        w = []
+        z = []
         for i in range(8):
             x = row_splat(sc, o + 64 + i)
-            y = row_splat(sc, o + 72 + i)
             for p in range(i):
-                x = x - low[i, p] * u[p]
-                y = y - low[i, p] * w[p]
-            u.append(x * inv[i])
-            w.append(y * inv[i])
-        u8 = u[7]
-        w8 = w[7]
+                x = x - low[i, p] * z[p]
+            z.append(x * inv[i])
+        z8 = z[7]
         for i in range(7):
-            u8 = jnp.where(sub == i, u[i], u8)
-            w8 = jnp.where(sub == i, w[i], w8)
-        u_ref[j:j + 8, :] = jnp.where(lane >= sub + j, u8, 0.0)
-        w_ref[j:j + 8, :] = jnp.where(lane < j + 8, w8, 0.0)
-        z = [jnp.where(lane < j + 8, w[i], u[i]) for i in range(8)]
+            z8 = jnp.where(sub == i, z[i], z8)
+        corner = jnp.zeros((8, SUB), F32)
+        for m in range(8):
+            x = d[m, m] * inv[m]
+            for i in range(m):
+                x = jnp.where(sub == i, low[m, i], x)
+            corner = jnp.where(lane == j + m, x, corner)
+        u_ref[j:j + 8, :] = jnp.where(lane >= j + 8, z8, jnp.where(lane >= sub + j, corner, 0.0))
+        w_ref[j:j + 8, :] = jnp.where(lane < j + 8, z8, 0.0)
         for s in range(t + 1, end):
             c = first if s == t + 1 else column(s)
             x = jnp.where((lane >= j) & (lane < j + 8), 0.0, X[s])
@@ -100,6 +98,7 @@
             X[s] = x
         if t + 1 == half:
             e = 8 * half
+            mid()
             top = u_ref[0:e, :]
             z = jnp.where(lax.broadcasted_iota(jnp.int32, (e, SUB), 1) < e, w_ref[0:e, :], top)
             prod = dot_hi(top[:, e:SUB], z, ((0,), (0,)))
@@ -214,7 +213,10 @@
         S[t, :, blk(s)] = S[t, :, blk(s)] - prod
 
     def fb_copy(slot, b):
-        view = FB.at[slot, b, :, SUB * b:BS]
+        if b < 2:
+            view = FB.at[slot, b, :, SUB * b:BS]
+        else:
+            view = FB.at[slot, 2, (b - 2) * SUB // 2:(b - 1) * SUB // 2, 2 * SUB:BS]
         return pltpu.make_async_remote_copy(view, view, fs_sem.at[slot, b], fr_sem.at[slot, b],
                                             device_id=to(1 - r, c), device_id_type=MESH)
 
@@ -256,9 +258,18 @@
     def factor_diag(slot, more, late):
         def tile(b, _):
             off = pl.multiple_of(b * SUB, SUB)
-            factor_tile(D, off, ub.at[b], wb, sc)
+            def mid():
+                @pl.when((b == 2) & more)
+                def _():
+                    FB[slot, 2, 0:SUB // 2, 2 * SUB:BS] = wb[0:SUB // 2, :]
+                    fb_copy(slot, 2).start()
+
+            factor_tile(D, off, ub.at[b], wb, sc, mid)
             w = wb[...]
-            FB[slot, b, :, pl.ds(off, SUB)] = w
+
+            @pl.when(b < 2)
+            def _():
+                FB[slot, b, :, pl.ds(off, SUB)] = w
 
             @pl.when(b == 0)
             def _():
@@ -283,7 +294,8 @@
             def _():
                 @pl.when(more)
                 def _():
-                    fb_copy(slot, 2).start()
+                    FB[slot, 2, SUB // 2:SUB, 2 * SUB:BS] = w[SUB // 2:SUB, :]
+                    fb_copy(slot, 3).start()
             return 0
         lax.fori_loop(0, 3, tile, 0)
 
@@ -400,6 +412,8 @@
                 if e == 1:
                     pass_on(n + 1 - HOP)
                 fb_copy(sd, e).wait_recv()
+                if e == 2:
+                    fb_copy(sd, 3).wait_recv()
             solve(kd, t, sd, ready, lambda e: near_copy(kd, e).start(), 3)
             each_send(kd, t, lambda cp: cp.start())
 
@@ -500,7 +514,7 @@
         def _():
             @pl.when(r == lax.rem(k, 2))
             def _():
-                for b in range(3):
+                for b in range(4):
                     fb_copy(k // 4, b).wait_send()
 
             @pl.when(r != lax.rem(k, 2))
@@ -529,8 +543,8 @@
                 pltpu.SemaphoreType.DMA((3, 64)),
                 pltpu.SemaphoreType.DMA((64,)),
                 pltpu.SemaphoreType.DMA((40,)),
-                pltpu.SemaphoreType.DMA((4, 3)),
-                pltpu.SemaphoreType.DMA((4, 3)),
+                pltpu.SemaphoreType.DMA((4, 4)),
+                pltpu.SemaphoreType.DMA((4, 4)),
                 pltpu.SemaphoreType.DMA((16, 5)),
                 pltpu.SemaphoreType.DMA((16, 5)),
             ],

time: 257 us -> 254 us (0.988)
  Pallas kernels: 250 us -> 247 us
    pallas_call x1, Pallas kernels: 250 us -> 247 us  [local(): pl.pallas_call(kernel, out_shape=pltpu.VMEM(a.shape, F32), in_specs=[pl.B...]
where the time goes in v6:
time: 254 us
  Pallas kernels  247 us (97%)
  local copies, waits for them, and re-layouts  6.85 us (3%)
    pallas_call x1, Pallas kernels, local(): pl.pallas_call(kernel, out_shape=pltpu.VMEM(a.shape, F32), in_specs=[pl.B...  247 us
    unnamed x1, local copies, waits for them, and re-layouts  6.85 us

profile of v6, /device:TPU:7, one launch (start us, length us, event | category | flops | bytes accessed | tf_op | source)
XLA Modules:
  0.0 253.8 jit_solution(6262788666339368116)
XLA Ops:
  0.0 247.0 %cholesky.1 = f32[8,384,1536]{2,1,0:T(8,128)S(1)} custom-call(f32[8,384,1536]{2,1,0:T(8,128)} %a_hbm.1), custom_call_target="tpu_custom_call" | custom-call | tf_op jit(solution)/shard_map/cholesky/pallas_call | solution.py:530
  247.0 6.9 %copy.3 = f32[8,384,1536]{2,1,0:T(8,128)} copy(f32[8,384,1536]{2,1,0:T(8,128)S(1)} %cholesky.1) | data formatting | bytes 37748736

commit v7 on v6

--- a/solution.py
+++ b/solution.py
@@ -307,8 +307,8 @@
 
         def put(n, x):
             PQ[idx, :, SUB * n:SUB * (n + 1)] = x.astype(BF16)
+            done(n)
             S[t, :, tile(n)] = x
-            done(n)
 
         ready(0)
         x1 = dot_hi(S[t, :, tile(0)], FB[s, 0, :, 0:SUB], ((1,), (1,)))
@@ -324,8 +324,8 @@
             at = slice(rows * h, rows * (h + 1))
             x3 = dot_hi(last[at], FB[s, 2, :, 2 * SUB:BS], ((1,), (1,)))
             PQ[idx, at, 2 * SUB:BS] = x3.astype(BF16)
+            done(2 + h)
             S[t, at, tile(2)] = x3
-            done(2 + h)
 
     def wave(n, _):
         kd = n // MU

time: 254 us -> 254 us (level)
  no operation moved by 1% of the time
where the time goes in v7:
time: 254 us
  Pallas kernels  247 us (97%)
  local copies, waits for them, and re-layouts  6.85 us (3%)
    pallas_call x1, Pallas kernels, local(): pl.pallas_call(kernel, out_shape=pltpu.VMEM(a.shape, F32), in_specs=[pl.B...  247 us
    unnamed x1, local copies, waits for them, and re-layouts  6.85 us

profile of v7, /device:TPU:7, one launch (start us, length us, event | category | flops | bytes accessed | tf_op | source)
XLA Modules:
  0.0 253.9 jit_solution(14695053673743432037)
XLA Ops:
  0.0 247.1 %cholesky.1 = f32[8,384,1536]{2,1,0:T(8,128)S(1)} custom-call(f32[8,384,1536]{2,1,0:T(8,128)} %a_hbm.1), custom_call_target="tpu_custom_call" | custom-call | tf_op jit(solution)/shard_map/cholesky/pallas_call | solution.py:530
  247.1 6.9 %copy.3 = f32[8,384,1536]{2,1,0:T(8,128)} copy(f32[8,384,1536]{2,1,0:T(8,128)S(1)} %cholesky.1) | data formatting | bytes 37748736
